TPU v7x, 32 devices: a whole 2x2x4 slice. The times are simulated.
32 devices in a mesh: dp: 4 (over z), tensor: 8 (over y, x, core).
Axes of the slice: x: 2, y: 2, z: 4, core: 2. Of those that a mesh axis runs over, the one named last changes fastest.
Arguments:
- layer_input: bfloat16 [16384, 2048], P(('dp', 'tensor')), may hold values from -20 to 20
- gain_attn: float32 [2048], replicated, may hold values from 0.25 to 1.75
- w_query: bfloat16 [2048, 2048], P(None, 'tensor'), may hold values from -0.125 to 0.125
- w_key: bfloat16 [2048, 2048], P(None, 'tensor'), may hold values from -0.125 to 0.125
- w_value: bfloat16 [2048, 2048], P(None, 'tensor'), may hold values from -0.125 to 0.125
- w_out: bfloat16 [2048, 2048], P('tensor'), may hold values from -1 to 1
- gain_mlp: float32 [2048], replicated, may hold values from 0.25 to 1.75
- w_gate: bfloat16 [2048, 8192], P(None, 'tensor'), may hold values from -0.125 to 0.125
- w_up: bfloat16 [2048, 8192], P(None, 'tensor'), may hold values from -0.125 to 0.125
- w_down: bfloat16 [8192, 2048], P('tensor'), may hold values from -0.0625 to 0.0625
- segment_ids: int32 [8, 2048], P('dp'), may hold values from 0 to 31, as said below
- positions: int32 [8, 2048], P('dp'), may hold values from 0 to 2047, as said below
- out_grad: bfloat16 [16384, 2048], P(('dp', 'tensor')), may hold values from -6 to 6
Outputs:
- layer_out: bfloat16 [16384, 2048], P(('dp', 'tensor'))
- input_grad: float32 [16384, 2048], P(('dp', 'tensor'))
- grad_gain_attn: float32 [2048], P('tensor')
- grad_w_query: float32 [2048, 2048], P(None, 'tensor')
- grad_w_key: float32 [2048, 2048], P(None, 'tensor')
- grad_w_value: float32 [2048, 2048], P(None, 'tensor')
- grad_w_out: float32 [2048, 2048], P('tensor')
- grad_gain_mlp: float32 [2048], P('tensor')
- grad_w_gate: float32 [2048, 8192], P(None, 'tensor')
- grad_w_up: float32 [2048, 8192], P(None, 'tensor')
- grad_w_down: float32 [8192, 2048], P('tensor')
Inputs may be any that keep to these rules, and one draw needn't show every extreme that they name: `segment_ids`: within each row the document number is 0 at the first token and rises by 0 or 1 from one token to the next; a row holds 1 to 32 documents; the first row of the batch is one document and the last row holds 32. `positions`: A position is 0 where a row begins or the document number changes, else one more than the position before.
All inputs are finite; a program needn't handle non-finite values.
Results may differ from a plain program's by a relative error of at most 0.024.
Values may be sent and summed in bfloat16 or wider, within the bound.
A program may use at most 320 MiB of HBM per device.

v0:
```python
import functools
import jax
import jax.numpy as jnp
from jax import lax
from jax.experimental import pallas as pl
from jax.experimental.pallas import tpu as pltpu
from jax.sharding import PartitionSpec as P


HD = 64
NEG = -1e30
NT = (((1,), (1,)), ((), ()))
VMEM_MAX = 60 * 1024 * 1024


def cost(flops, nbytes):
    return pl.CostEstimate(flops=flops, bytes_accessed=nbytes, transcendentals=0)


def swap_halves(values):
    width = values.shape[-1]
    if width == HD:
        return jnp.concatenate([values[:, HD // 2 :], values[:, : HD // 2]], axis=1)
    lane = lax.broadcasted_iota(jnp.int32, values.shape, 1)
    return jnp.where(
        lane % HD < HD // 2,
        pltpu.roll(values, width - HD // 2, 1),
        pltpu.roll(values, HD // 2, 1),
    )


def turn(values, cosine, sine):
    width = cosine.shape[-1]
    parts = []
    for start in range(0, values.shape[-1], width):
        piece = values[:, start : start + width]
        parts.append(piece * cosine + swap_halves(piece) * sine)
    return parts[0] if len(parts) == 1 else jnp.concatenate(parts, axis=1)


def turn_back(values, cosine, sine):
    width = cosine.shape[-1]
    parts = []
    for start in range(0, values.shape[-1], width):
        piece = values[:, start : start + width]
        parts.append(piece * cosine + swap_halves(piece * sine))
    return parts[0] if len(parts) == 1 else jnp.concatenate(parts, axis=1)


def qkv_kernel(x_ref, w_ref, cos_ref, sin_ref, q_ref, k_ref, v_ref):
    width = q_ref.shape[1]
    projected = jnp.dot(x_ref[...], w_ref[...], preferred_element_type=jnp.float32)
    cosine, sine = cos_ref[...], sin_ref[...]
    turned = turn(projected[:, :width], cosine, sine).astype(jnp.bfloat16)
    q_ref[...] = turned * jnp.bfloat16(HD**-0.5)
    k_ref[...] = turn(projected[:, width : 2 * width], cosine, sine).astype(jnp.bfloat16)
    v_ref[...] = projected[:, 2 * width :].astype(jnp.bfloat16)


def project(tokens, joined_w, cosine, sine):
    count, depth = tokens.shape
    width = joined_w.shape[1] // 3
    block = min(512, count)
    rows = lambda i: (i, 0)
    out = jax.ShapeDtypeStruct((count, width), jnp.bfloat16)
    return pl.pallas_call(
        qkv_kernel,
        grid=(count // block,),
        in_specs=[
            pl.BlockSpec((block, depth), rows),
            pl.BlockSpec((depth, 3 * width), lambda i: (0, 0), pipeline_mode=pl.Buffered(1)),
            pl.BlockSpec((block, cosine.shape[1]), rows),
            pl.BlockSpec((block, cosine.shape[1]), rows),
        ],
        out_specs=[pl.BlockSpec((block, width), rows)] * 3,
        out_shape=[out] * 3,
        compiler_params=pltpu.CompilerParams(vmem_limit_bytes=VMEM_MAX),
        cost_estimate=cost(6 * count * depth * width, 2 * count * depth),
        name="qkv",
    )(tokens, joined_w, cosine, sine)


def head_parts(values):
    heads = values.shape[1] // HD
    if heads == 1:
        return [values]
    lane = lax.broadcasted_iota(jnp.int32, values.shape, 1) // HD
    return [jnp.where(lane == h, values, jnp.zeros_like(values)) for h in range(heads)]


def forward_kernel(bk, low_ref, q_ref, k_ref, v_ref, pos_ref, o_ref, lse_ref, vt, acc, top, total):
    row, i = pl.program_id(0), pl.program_id(1)
    bq, width = q_ref.shape
    heads = width // HD

    @pl.when(i == 0)
    def _():
        vt[...] = v_ref[...].T

    q_parts = head_parts(q_ref[...])
    q_index = i * bq + lax.broadcasted_iota(jnp.int32, (1, bq), 1)
    first = q_index - pos_ref[0]
    acc[...] = jnp.zeros_like(acc)
    top[...] = jnp.full_like(top, NEG)
    total[...] = jnp.zeros_like(total)

    def step(j, carry):
        at = pl.ds(pl.multiple_of(j * bk, bk), bk)
        keys = k_ref[at, :]
        k_index = j * bk + lax.broadcasted_iota(jnp.int32, (bk, bq), 0)
        allowed = (k_index >= first) & (k_index <= q_index)
        for h in range(heads):
            mine = slice(h * HD, (h + 1) * HD)
            scores = lax.dot_general(keys, q_parts[h], NT, preferred_element_type=jnp.float32)
            scores = jnp.where(allowed, scores, NEG)
            old = top[h : h + 1, :]
            new = jnp.maximum(old, jnp.max(scores, axis=0, keepdims=True))
            probs = jnp.exp(scores - new)
            fade = jnp.exp(old - new)
            top[h : h + 1, :] = new
            total[h : h + 1, :] = fade * total[h : h + 1, :] + jnp.sum(probs, axis=0, keepdims=True)
            acc[mine, :] = fade * acc[mine, :] + jnp.dot(
                vt[mine, at], probs.astype(jnp.bfloat16), preferred_element_type=jnp.float32
            )
        return carry

    lax.fori_loop(low_ref[row, i], ((i + 1) * bq + bk - 1) // bk, step, 0)
    for h in range(heads):
        mine = slice(h * HD, (h + 1) * HD)
        acc[mine, :] = acc[mine, :] / total[h : h + 1, :]
    o_ref[...] = acc[...].T.astype(jnp.bfloat16)
    lse_ref[0] = top[...] + jnp.log(jnp.maximum(total[...], 1e-30))


def attend_forward(q, k, v, positions, bq, bk):
    rows, length = positions.shape
    width = q.shape[1]
    per = length // bq
    starts = jnp.arange(0, length, bq, dtype=jnp.int32)
    low = (starts[None, :] - positions[:, ::bq]) // bk
    pos3 = positions[:, None, :]
    return pl.pallas_call(
        functools.partial(forward_kernel, bk),
        grid_spec=pltpu.PrefetchScalarGridSpec(
            num_scalar_prefetch=1,
            grid=(rows, per),
            in_specs=[
                pl.BlockSpec((bq, width), lambda r, i, low: (r * per + i, 0)),
                pl.BlockSpec((length, width), lambda r, i, low: (r, 0)),
                pl.BlockSpec((length, width), lambda r, i, low: (r, 0)),
                pl.BlockSpec((1, 1, bq), lambda r, i, low: (r, 0, i)),
            ],
            out_specs=[
                pl.BlockSpec((bq, width), lambda r, i, low: (r * per + i, 0)),
                pl.BlockSpec((1, 8, bq), lambda r, i, low: (r, 0, i)),
            ],
            scratch_shapes=[
                pltpu.VMEM((width, length), jnp.bfloat16),
                pltpu.VMEM((width, bq), jnp.float32),
                pltpu.VMEM((8, bq), jnp.float32),
                pltpu.VMEM((8, bq), jnp.float32),
            ],
        ),
        out_shape=[
            jax.ShapeDtypeStruct((rows * length, width), jnp.bfloat16),
            jax.ShapeDtypeStruct((rows, 8, length), jnp.float32),
        ],
        compiler_params=pltpu.CompilerParams(vmem_limit_bytes=VMEM_MAX),
        cost_estimate=cost(16 * rows * length * length * width, 10 * rows * length * width),
        name="attend",
    )(low, q, k, v, pos3)


def backward_kernel(
    bk, bq, low_ref, q_ref, k_ref, v_ref, o_ref, do_ref, lse_ref, pos_ref, cos_ref, sin_ref, out_ref,
    kt, dqt, dk, dv,
):
    row, i = pl.program_id(0), pl.program_id(1)
    width = q_ref.shape[1]
    heads = width // HD
    here = pl.ds(pl.multiple_of(i * bq, bq), bq)

    @pl.when(i == 0)
    def _():
        kt[...] = k_ref[...].T
        dk[...] = jnp.zeros_like(dk)
        dv[...] = jnp.zeros_like(dv)

    grads = do_ref[here, :]
    q_parts = head_parts(q_ref[here, :])
    g_parts = head_parts(grads)
    stacked_q = jnp.concatenate(q_parts, axis=0)
    stacked_g = jnp.concatenate(g_parts, axis=0)
    products = grads.astype(jnp.float32) * o_ref[here, :].astype(jnp.float32)
    pick = (
        lax.broadcasted_iota(jnp.int32, (8, width), 1) // HD
        == lax.broadcasted_iota(jnp.int32, (8, width), 0)
    ).astype(jnp.float32)
    centre = lax.dot_general(
        pick, products, NT, precision=lax.Precision.HIGHEST, preferred_element_type=jnp.float32
    )
    level = lse_ref[0, :, here]
    q_index = i * bq + lax.broadcasted_iota(jnp.int32, (1, bq), 1)
    first = q_index - pos_ref[0, :, here]
    dqt[...] = jnp.zeros_like(dqt)

    def step(j, carry):
        at = pl.ds(pl.multiple_of(j * bk, bk), bk)
        keys, values = k_ref[at, :], v_ref[at, :]
        k_index = j * bk + lax.broadcasted_iota(jnp.int32, (bk, bq), 0)
        allowed = (k_index >= first) & (k_index <= q_index)
        all_p, all_s = [], []
        for h in range(heads):
            mine = slice(h * HD, (h + 1) * HD)
            scores = lax.dot_general(keys, q_parts[h], NT, preferred_element_type=jnp.float32)
            probs = jnp.where(allowed, jnp.exp(scores - level[h : h + 1, :]), 0.0)
            d_probs = lax.dot_general(values, g_parts[h], NT, preferred_element_type=jnp.float32)
            d_scores = (probs * (d_probs - centre[h : h + 1, :])).astype(jnp.bfloat16)
            dqt[mine, :] += jnp.dot(kt[mine, at], d_scores, preferred_element_type=jnp.float32)
            all_p.append(probs.astype(jnp.bfloat16))
            all_s.append(d_scores)
        dv[at, :] += jnp.dot(
            jnp.concatenate(all_p, axis=1), stacked_g, preferred_element_type=jnp.float32
        )
        dk[at, :] += jnp.dot(
            jnp.concatenate(all_s, axis=1), stacked_q, preferred_element_type=jnp.float32
        )
        return carry

    lax.fori_loop(low_ref[row, i], ((i + 1) * bq + bk - 1) // bk, step, 0)
    out_ref[here, 0:width] = turn_back(
        dqt[...].T * (HD**-0.5), cos_ref[here, :], sin_ref[here, :]
    ).astype(jnp.bfloat16)

    @pl.when(i == pl.num_programs(1) - 1)
    def _():
        out_ref[:, width : 2 * width] = turn_back(dk[...], cos_ref[...], sin_ref[...]).astype(
            jnp.bfloat16
        )
        out_ref[:, 2 * width : 3 * width] = dv[...].astype(jnp.bfloat16)


def attend_backward(row, so_far, q, k, v, o, d_o, lse, positions, cosine, sine, bq, bk):
    rows, length = positions.shape
    width = q.shape[1]
    per = length // bq
    starts = jnp.arange(0, length, bq, dtype=jnp.int32)
    low = (starts[None, :] - positions[row : row + 1, ::bq]) // bk
    pos3 = positions[:, None, :]
    whole = pl.BlockSpec((length, width), lambda r, i, low: (row, 0))
    table = pl.BlockSpec((length, cosine.shape[1]), lambda r, i, low: (row, 0))
    arrays = [low, q, k, v, o, d_o, lse, pos3, cosine, sine]
    specs = [whole] * 5 + [
        pl.BlockSpec((1, 8, length), lambda r, i, low: (row, 0, 0)),
        pl.BlockSpec((1, 1, length), lambda r, i, low: (row, 0, 0)),
        table,
        table,
    ]
    body, alias = functools.partial(backward_kernel, bk, bq), {}
    if so_far is not None:
        arrays.append(so_far)
        specs.append(pl.BlockSpec(memory_space=pl.ANY))
        alias = {len(arrays) - 1: 0}
        body = lambda *refs: backward_kernel(bk, bq, *refs[:10], *refs[11:])
    return pl.pallas_call(
        body,
        grid_spec=pltpu.PrefetchScalarGridSpec(
            num_scalar_prefetch=1,
            grid=(1, per),
            in_specs=specs,
            out_specs=pl.BlockSpec((length, 3 * width), lambda r, i, low: (row, 0)),
            scratch_shapes=[
                pltpu.VMEM((width, length), jnp.bfloat16),
                pltpu.VMEM((width, bq), jnp.float32),
                pltpu.VMEM((length, width), jnp.float32),
                pltpu.VMEM((length, width), jnp.float32),
            ],
        ),
        out_shape=jax.ShapeDtypeStruct((rows * length, 3 * width), jnp.bfloat16),
        input_output_aliases=alias,
        compiler_params=pltpu.CompilerParams(vmem_limit_bytes=VMEM_MAX),
        cost_estimate=cost(28 * length * length * width, 20 * length * width),
        name="attend_back",
    )(*arrays)


def mlp_kernel(n_ref, g_ref, wg_ref, wu_ref, wd_ref, hidden_ref, both_ref):
    ff = hidden_ref.shape[1]
    tokens = n_ref[...]
    gate = jnp.dot(tokens, wg_ref[...], preferred_element_type=jnp.float32)
    up = jnp.dot(tokens, wu_ref[...], preferred_element_type=jnp.float32)
    d_hidden = lax.dot_general(g_ref[...], wd_ref[...], NT, preferred_element_type=jnp.float32)
    sig = 1.0 / (1.0 + jnp.exp(-gate))
    act = gate * sig
    hidden_ref[...] = (act * up).astype(jnp.bfloat16)
    both_ref[:, ff:] = (d_hidden * act).astype(jnp.bfloat16)
    both_ref[:, :ff] = (d_hidden * up * (sig * (1.0 + gate * (1.0 - sig)))).astype(jnp.bfloat16)


def mlp_middle(tokens, grads, w_gate, w_up, w_down, block=256):
    count, depth = tokens.shape
    ff = w_gate.shape[1]
    block = min(block, count)
    rows = lambda i: (i, 0)
    fixed = lambda i: (0, 0)
    one = pl.Buffered(1)
    return pl.pallas_call(
        mlp_kernel,
        grid=(count // block,),
        in_specs=[
            pl.BlockSpec((block, depth), rows),
            pl.BlockSpec((block, depth), rows),
            pl.BlockSpec((depth, ff), fixed, pipeline_mode=one),
            pl.BlockSpec((depth, ff), fixed, pipeline_mode=one),
            pl.BlockSpec((ff, depth), fixed, pipeline_mode=one),
        ],
        out_specs=[pl.BlockSpec((block, ff), rows), pl.BlockSpec((block, 2 * ff), rows)],
        out_shape=[
            jax.ShapeDtypeStruct((count, ff), jnp.bfloat16),
            jax.ShapeDtypeStruct((count, 2 * ff), jnp.bfloat16),
        ],
        compiler_params=pltpu.CompilerParams(vmem_limit_bytes=VMEM_MAX),
        cost_estimate=cost(6 * count * depth * ff, 4 * count * depth),
        name="mlp_middle",
    )(tokens, grads, w_gate, w_up, w_down)


rope_theta = 130000.0
norm_eps = 1e-05


def rotary_tables(position_list, width):
    half_dim = HD // 2
    frequency = rope_theta ** (-(jnp.arange(half_dim, dtype=jnp.float32) * 2.0 / HD))
    angles = position_list.astype(jnp.float32)[:, None] * frequency[None, :]
    cosine, sine = jnp.cos(angles), jnp.sin(angles)
    times = width // HD
    return (
        jnp.concatenate([cosine, cosine] * times, axis=1),
        jnp.concatenate([-sine, sine] * times, axis=1),
    )


def normalize(row_values):
    inverse = lax.rsqrt(jnp.mean(row_values * row_values, axis=-1, keepdims=True) + norm_eps)
    return (row_values * inverse, inverse)


def norm_back(grad_in, gain_vec, unit_rows, inverse):
    scaled = grad_in * gain_vec
    return inverse * (scaled - unit_rows * jnp.mean(scaled * unit_rows, axis=-1, keepdims=True))


def hop(piece, moves):
    return lax.ppermute(piece, "dp", moves)


def sum_over_dp(piece):
    if lax.axis_size("dp") != 4:
        return lax.psum(piece, "dp").astype(jnp.float32)
    place = lax.axis_index("dp")
    inner = (place == 1) | (place == 2)
    pair = piece + hop(piece, [(0, 1), (3, 2)])
    whole = pair + hop(pair, [(1, 2), (2, 1)])
    arrived = hop(whole, [(1, 0), (2, 3)])
    return jnp.where(inner, whole, arrived).astype(jnp.float32)


def local(
    layer_input,
    gain_attn,
    w_query,
    w_key,
    w_value,
    w_out,
    gain_mlp,
    w_gate,
    w_up,
    w_down,
    segment_ids,
    positions,
    out_grad,
):
    width = layer_input.shape[1]
    hidden_w = w_query.shape[1]
    ff_local = w_gate.shape[1]
    length = positions.shape[1]
    bf16, f32 = jnp.bfloat16, jnp.float32
    block = min(512, length)

    def gather(value):
        return lax.all_gather(value, "tensor", axis=0, tiled=True)

    def scatter(value):
        return lax.psum_scatter(value, "tensor", scatter_dimension=0, tiled=True)

    def mm(a, b, dims=(((1,), (0,)), ((), ()))):
        return lax.dot_general(a, b, dims, preferred_element_type=f32)

    TN = (((0,), (0,)), ((), ()))
    joined_w = jnp.concatenate([w_query, w_key, w_value], axis=1)
    both_w = jnp.concatenate([w_gate, w_up], axis=1)
    cosine, sine = rotary_tables(positions.reshape(-1), min(2 * HD, hidden_w))

    inputs = layer_input.astype(f32)
    unit_one, inverse_one = normalize(inputs)
    all_one = gather((unit_one * gain_attn).astype(bf16))
    all_grad = gather(out_grad)
    all_w_out = gather(w_out)
    queries, keys, values = project(all_one, joined_w, cosine, sine)
    attended, level = attend_forward(queries, keys, values, positions, block, block)
    mixed = lax.all_to_all(attended, "tensor", split_axis=0, concat_axis=1, tiled=True)
    residual = inputs + mm(mixed, all_w_out)

    unit_two, inverse_two = normalize(residual)
    all_two = gather((unit_two * gain_mlp).astype(bf16))
    hidden, d_both = mlp_middle(all_two, all_grad, w_gate, w_up, w_down)
    grad_down = mm(hidden, all_grad, TN).astype(bf16)
    d_two = scatter(mm(d_both, both_w, NT).astype(bf16)).astype(f32)
    grad_gate = mm(all_two, d_both[:, :ff_local], TN).astype(bf16)
    grad_up = mm(all_two, d_both[:, ff_local:], TN).astype(bf16)
    layer_sum = scatter(mm(hidden, w_down).astype(bf16))

    gain_two_part = jnp.sum(d_two * unit_two, axis=0)
    d_residual = out_grad.astype(f32) + norm_back(d_two, gain_mlp, unit_two, inverse_two)
    d_attn = d_residual.astype(bf16)
    d_mixed = mm(d_attn, all_w_out, NT).astype(bf16)
    d_attended = lax.all_to_all(d_mixed, "tensor", split_axis=1, concat_axis=0, tiled=True)
    grad_out = scatter(mm(mixed, d_attn, TN).astype(bf16))
    d_projected = None
    for row in range(positions.shape[0]):
        d_projected = attend_backward(
            row, d_projected, queries, keys, values, attended, d_attended, level, positions,
            cosine, sine, block, block,
        )
    layer_sum, d_projected = lax.optimization_barrier((layer_sum, d_projected))
    layer_out = (residual + layer_sum.astype(f32)).astype(bf16)
    d_one = scatter(mm(d_projected, joined_w, NT).astype(bf16)).astype(f32)
    grad_joined = mm(all_one, d_projected, TN).astype(bf16)
    plain_joined = lax.optimization_barrier(grad_joined)
    gain_one_part = jnp.sum(plain_joined.astype(f32) * joined_w.astype(f32), axis=1) / gain_attn
    gains = lax.psum_scatter(
        jnp.stack([gain_one_part, gain_two_part]), "tensor", scatter_dimension=1, tiled=True
    )
    gains = sum_over_dp(gains)
    input_grad = d_residual + norm_back(d_one, gain_attn, unit_one, inverse_one)

    down = sum_over_dp(grad_down)
    gate = sum_over_dp(grad_gate)
    up = sum_over_dp(grad_up)
    rest = jnp.concatenate([grad_joined, grad_out.reshape(width, hidden_w)], axis=1)
    middle = width // 2
    rest = jnp.concatenate([sum_over_dp(rest[:middle]), sum_over_dp(rest[middle:])], axis=0)
    return (
        layer_out,
        input_grad,
        gains[0],
        rest[:, :hidden_w],
        rest[:, hidden_w : 2 * hidden_w],
        rest[:, 2 * hidden_w : 3 * hidden_w],
        rest[:, 3 * hidden_w :].reshape(hidden_w, width),
        gains[1],
        gate,
        up,
        down,
    )


def solution(mesh):
    return jax.shard_map(
        local,
        mesh=mesh,
        in_specs=(
            P(("dp", "tensor"), None),
            P(),
            P(None, "tensor"),
            P(None, "tensor"),
            P(None, "tensor"),
            P("tensor", None),
            P(),
            P(None, "tensor"),
            P(None, "tensor"),
            P("tensor", None),
            P("dp", None),
            P("dp", None),
            P(("dp", "tensor"), None),
        ),
        out_specs=(
            P(("dp", "tensor"), None),
            P(("dp", "tensor"), None),
            P("tensor"),
            P(None, "tensor"),
            P(None, "tensor"),
            P(None, "tensor"),
            P("tensor", None),
            P("tensor"),
            P(None, "tensor"),
            P(None, "tensor"),
            P("tensor", None),
        ),
        check_vma=False,
    )
```

profile of v0, /device:TPU:0, one launch (start us, length us, event | category | flops | bytes accessed | tf_op | source)
XLA Modules:
  0.0 1489.5 jit_solution(564897245811649570)
XLA Ops:
  32.9 73.1 %all-gather.5.cloned.1.call-done.x_ref = bf16[4096,2048]{1,0:T(8,128)(2,1)} async-done(((bf16[512,2048]{1,0:T(8,128)(2,1)}), bf16[4096,2048]{1,0:T(8,128)(2,1)}) %all-gather.5.cloned.1.call-update) | async-done | bytes 16777232 | tf_op jit(solution)/shard_map/all_gather | solution.py:392
  106.0 19.9 %qkv.1 = (bf16[4096,256]{1,0:T(8,128)(2,1)}, bf16[4096,256]{1,0:T(8,128)(2,1)}, bf16[4096,256]{1,0:T(8,128)(2,1)}) custom-call(bf16[4096,2048]{1,0:T(8,128)(2,1)} %all-gather.5.cloned.1.call-done.x_ref, bf16[2048,768]{1,0:T(8,128)(2,1)} %copy-done.8, f32[4096,128]{1,0:T(8,128)} %get-tuple-element.44.cos_ref.refs_8_, ...), custom_call_target="tpu_custom_call" | custom-call | flops 12884901888 | bytes 16777216 | tf_op jit(solution)/shard_map/qkv/pallas_call | solution.py:66
  126.0 53.0 %attend.1 = (bf16[4096,256]{1,0:T(8,128)(2,1)}, f32[2,8,2048]{2,1,0:T(8,128)}) custom-call(s32[2,4]{1,0:T(2,128)} %and_select_fusion.2.low_ref, bf16[4096,256]{1,0:T(8,128)(2,1)} %get-tuple-element.20.q_ref.refs_1_, bf16[4096,256]{1,0:T(8,128)(2,1)} %get-tuple-element.21.k_ref.refs_2_, bf16[4096,256]{1,0:T(8,128)(2,1)} %get-tuple-element.22.v_ref.refs_3_, ...), custom_call_target="tpu_custom_call" | custom-call | flops 34359738368 | bytes 10485760 | tf_op jit(solution)/shard_map/attend/pallas_call | solution.py:142
  188.0 33.8 %all-to-all-done = bf16[8,512,256]{1,2,0:T(8,128)(2,1)} async-done(((bf16[8,512,256]{1,2,0:T(8,128)(2,1)}), bf16[8,512,256]{1,2,0:T(8,128)(2,1)}, u32[]{:S(2)}, u32[]{:S(2)}) %all-to-all-start) | async-done | bytes 2097184 | tf_op jit(solution)/shard_map/all_to_all | solution.py:412
  221.8 7.8 multiply_reduce_fusion.1
  233.4 42.9 %all-gather.11.cloned.1.call-done.g_ref = bf16[4096,2048]{1,0:T(8,128)(2,1)} async-done(((bf16[512,2048]{1,0:T(8,128)(2,1)}), bf16[4096,2048]{1,0:T(8,128)(2,1)}) %all-gather.11.cloned.1.call-update) | async-done | bytes 16777232 | tf_op jit(solution)/shard_map/all_gather | solution.py:392
  276.3 92.1 %all-gather.9.cloned.1.call-done.n_ref = bf16[4096,2048]{1,0:T(8,128)(2,1)} async-done(((bf16[512,2048]{1,0:T(8,128)(2,1)}), bf16[4096,2048]{1,0:T(8,128)(2,1)}) %all-gather.9.cloned.1.call-update) | async-done | bytes 16777232 | tf_op jit(solution)/shard_map/all_gather | solution.py:392
  368.4 62.6 %mlp_middle.1 = (bf16[4096,1024]{1,0:T(8,128)(2,1)}, bf16[4096,2048]{1,0:T(8,128)(2,1)}) custom-call(bf16[4096,2048]{1,0:T(8,128)(2,1)} %all-gather.9.cloned.1.call-done.n_ref, bf16[4096,2048]{1,0:T(8,128)(2,1)} %all-gather.11.cloned.1.call-done.g_ref, bf16[2048,1024]{1,0:T(8,128)(2,1)} %wg_ref.1, bf16[2048,1024]{1,0:T(8,128)(2,1)} %wu_ref.1, ...), custom_call_target="tpu_custom_call" | custom-call | flops 51539607552 | bytes 33554432 | tf_op jit(solution)/shard_map/mlp_middle/pallas_call | solution.py:307
  431.0 42.0 %convolution_convert_fusion.2 = bf16[4096,2048]{1,0:T(8,128)(2,1)} fusion(bf16[4096,2048]{1,0:T(8,128)(2,1)} %get-tuple-element.25, bf16[2048,1024]{1,0:T(8,128)(2,1)} %wu_ref.1, bf16[2048,1024]{1,0:T(8,128)(2,1)} %wg_ref.1), kind=kOutput, calls=%fused_computation.2 | convolution fusion | flops 34384904192 | bytes 41943040 | tf_op jit(solution)/shard_map/dot_general | solution.py:398
  473.3 24.1 %convolution_convert_fusion.1 = bf16[4096,2048]{1,0:T(8,128)(2,1)} fusion(bf16[4096,1024]{1,0:T(8,128)(2,1)} %get-tuple-element.24, bf16[1024,2048]{1,0:T(8,128)(2,1)} %wd_ref.1), kind=kOutput, calls=%fused_computation.1 | convolution fusion | flops 17188257792 | bytes 29360128 | tf_op jit(solution)/shard_map/dot_general | solution.py:398
  497.5 91.9 %reduce-scatter.10.cloned.1.call-done = bf16[512,2048]{1,0:T(8,128)(2,1)} async-done(((bf16[4096,2048]{1,0:T(8,128)(2,1)}), bf16[512,2048]{1,0:T(8,128)(2,1)}) %reduce-scatter.10.cloned.1.call-update) | async-done | bytes 2097168 | tf_op jit(solution)/shard_map/reduce_scatter | solution.py:395
  598.5 8.7 convolution_convert_fusion.3
  607.2 11.5 convolution_convert_fusion.6
  626.7 42.1 %all-to-all-done.1 = bf16[512,8,256]{2,0,1:T(8,128)(2,1)S(1)} async-done(((bf16[512,8,256]{2,0,1:T(8,128)(2,1)}), bf16[512,8,256]{2,0,1:T(8,128)(2,1)S(1)}, u32[]{:S(2)}, u32[]{:S(2)}) %all-to-all-start.1) | async-done | bytes 2097184 | tf_op jit(solution)/shard_map/all_to_all | solution.py:428
  670.1 48.6 %attend_back.2.refs_10_ = bf16[4096,768]{1,0:T(8,128)(2,1)} custom-call(s32[1,4]{1,0:T(1,128)} %and_select_fusion.low_ref, bf16[4096,256]{1,0:T(8,128)(2,1)} %get-tuple-element.20.q_ref.refs_1_, bf16[4096,256]{1,0:T(8,128)(2,1)} %get-tuple-element.21.k_ref.refs_2_, bf16[4096,256]{1,0:T(8,128)(2,1)} %get-tuple-element.22.v_ref.refs_3_, ...), custom_call_target="tpu_custom_call" | custom-call | flops 30064771072 | bytes 10485760 | tf_op jit(solution)/shard_map/attend_back/pallas_call | solution.py:265
  718.7 41.4 %attend_back.3 = bf16[4096,768]{1,0:T(8,128)(2,1)} custom-call(s32[1,4]{1,0:T(1,128)} %and_select_fusion.1.refs_0_, bf16[4096,256]{1,0:T(8,128)(2,1)} %get-tuple-element.20.q_ref.refs_1_, bf16[4096,256]{1,0:T(8,128)(2,1)} %get-tuple-element.21.k_ref.refs_2_, bf16[4096,256]{1,0:T(8,128)(2,1)} %get-tuple-element.22.v_ref.refs_3_, ...), custom_call_target="tpu_custom_call", output_to_operand_aliasing={{}: (10, {})} | custom-call | flops 30064771072 | bytes 10485760 | tf_op jit(solution)/shard_map/attend_back/pallas_call | solution.py:265
  760.2 19.9 %convolution_convert_fusion.5 = bf16[2048,768]{1,0:T(8,128)(2,1)S(1)} fusion(bf16[4096,2048]{1,0:T(8,128)(2,1)} %all-gather.5.cloned.1.call-done.x_ref, bf16[4096,768]{1,0:T(8,128)(2,1)} %attend_back.3), kind=kOutput, calls=%fused_computation.45 | convolution fusion | flops 12886474752 | bytes 26214400 | tf_op jit(solution)/shard_map/dot_general | solution.py:398
  782.4 20.3 %convolution_convert_fusion = bf16[4096,2048]{1,0:T(8,128)(2,1)} fusion(bf16[4096,768]{1,0:T(8,128)(2,1)} %attend_back.3, bf16[2048,768]{1,0:T(8,128)(2,1)} %copy-done.8), kind=kOutput, calls=%fused_computation | convolution fusion | flops 12893290496 | bytes 26214400 | tf_op jit(solution)/shard_map/dot_general | solution.py:398
  802.7 22.7 %fusion.22 = bf16[2048,1024]{1,0:T(8,128)(2,1)S(1)} fusion(bf16[4096,2048]{1,0:T(8,128)(2,1)} %all-gather.9.cloned.1.call-done.n_ref, bf16[4096,2048]{1,0:T(8,128)(2,1)} %get-tuple-element.25), kind=kOutput, calls=%fused_computation.42 | convolution fusion | flops 17181966336 | bytes 29360128 | tf_op jit(solution)/shard_map/dot_general | solution.py:398
  828.8 23.1 %fusion.25 = bf16[2048,1024]{1,0:T(8,128)(2,1)S(1)} fusion(bf16[4096,2048]{1,0:T(8,128)(2,1)} %all-gather.9.cloned.1.call-done.n_ref, bf16[4096,2048]{1,0:T(8,128)(2,1)} %get-tuple-element.25), kind=kOutput, calls=%fused_computation.43 | convolution fusion | flops 17181966336 | bytes 29360128 | tf_op jit(solution)/shard_map/dot_general | solution.py:398
  855.5 25.1 %convolution_convert_fusion.4 = bf16[1024,2048]{1,0:T(8,128)(2,1)S(1)} fusion(bf16[4096,1024]{1,0:T(8,128)(2,1)} %get-tuple-element.24, bf16[4096,2048]{1,0:T(8,128)(2,1)} %all-gather.11.cloned.1.call-done.g_ref), kind=kOutput, calls=%fused_computation.44 | convolution fusion | flops 17181966336 | bytes 29360128 | tf_op jit(solution)/shard_map/dot_general | solution.py:398
  882.2 35.5 %collective-permute-done.9 = bf16[2048,1024]{1,0:T(8,128)(2,1)} collective-permute-done((bf16[2048,1024]{1,0:T(8,128)(2,1)S(1)}, bf16[2048,1024]{1,0:T(8,128)(2,1)}, u32[]{:S(2)}, u32[]{:S(2)}) %collective-permute-start.9) | collective-permute-done | bytes 4194336 | tf_op jit(solution)/shard_map/ppermute | solution.py:355
  926.2 81.4 %collective-permute-done.12 = bf16[2048,1024]{1,0:T(8,128)(2,1)} collective-permute-done((bf16[2048,1024]{1,0:T(8,128)(2,1)S(1)}, bf16[2048,1024]{1,0:T(8,128)(2,1)}, u32[]{:S(2)}, u32[]{:S(2)}) %collective-permute-start.12) | collective-permute-done | bytes 4194336 | tf_op jit(solution)/shard_map/ppermute | solution.py:355
  1017.0 76.3 %collective-permute-done.15 = bf16[1024,2048]{1,0:T(8,128)(2,1)S(1)} collective-permute-done((bf16[1024,2048]{1,0:T(8,128)(2,1)S(1)}, bf16[1024,2048]{1,0:T(8,128)(2,1)S(1)}, u32[]{:S(2)}, u32[]{:S(2)}) %collective-permute-start.15) | collective-permute-done | bytes 4194336 | tf_op jit(solution)/shard_map/ppermute | solution.py:355
  1118.3 7.6 add.92
  1133.9 7.8 add.94
  1143.0 21.1 %collective-permute-done.3 = bf16[1024,1024]{1,0:T(8,128)(2,1)S(1)} collective-permute-done((bf16[1024,1024]{1,0:T(8,128)(2,1)S(1)}, bf16[1024,1024]{1,0:T(8,128)(2,1)S(1)}, u32[]{:S(2)}, u32[]{:S(2)}) %collective-permute-start.3) | collective-permute-done | bytes 2097184 | tf_op jit(solution)/shard_map/ppermute | solution.py:355
  1168.5 35.3 %collective-permute-done.6 = bf16[1024,1024]{1,0:T(8,128)(2,1)S(1)} collective-permute-done((bf16[1024,1024]{1,0:T(8,128)(2,1)S(1)}, bf16[1024,1024]{1,0:T(8,128)(2,1)S(1)}, u32[]{:S(2)}, u32[]{:S(2)}) %collective-permute-start.6) | collective-permute-done | bytes 2097184 | tf_op jit(solution)/shard_map/ppermute | solution.py:355
  1214.2 8.1 collective-permute-start
  1226.8 65.1 %collective-permute-done.14 = bf16[2048,1024]{1,0:T(8,128)(2,1)} collective-permute-done((bf16[2048,1024]{1,0:T(8,128)(2,1)}, bf16[2048,1024]{1,0:T(8,128)(2,1)}, u32[]{:S(2)}, u32[]{:S(2)}) %collective-permute-start.14) | collective-permute-done | bytes 4194336 | tf_op jit(solution)/shard_map/ppermute | solution.py:355
  1302.8 78.9 %collective-permute-done.17 = bf16[1024,2048]{1,0:T(8,128)(2,1)} collective-permute-done((bf16[1024,2048]{1,0:T(8,128)(2,1)}, bf16[1024,2048]{1,0:T(8,128)(2,1)}, u32[]{:S(2)}, u32[]{:S(2)}) %collective-permute-start.17) | collective-permute-done | bytes 4194336 | tf_op jit(solution)/shard_map/ppermute | solution.py:355
  1391.2 75.3 %collective-permute-done.2 = f32[2,256]{1,0:T(2,128)S(1)} collective-permute-done((f32[2,256]{1,0:T(2,128)S(1)}, f32[2,256]{1,0:T(2,128)S(1)}, u32[]{:S(2)}, u32[]{:S(2)}) %collective-permute-start.2) | collective-permute-done | bytes 2080 | tf_op jit(solution)/shard_map/ppermute | solution.py:355
  (153 shorter events, 175.7 us)
Async XLA Ops:
  7.2 98.8 %all-gather.5.cloned.1.call-start = ((), (), s32[]{:S(2)}) async-start(), calls=%async_computation.7 | async-start | bytes 18874368 | tf_op jit(solution)/shard_map/all_gather | solution.py:392
  13.4 174.6 %all-gather.7.cloned.1.call-start = ((), (), s32[]{:S(2)}) async-start(), calls=%async_computation.8 | async-start | bytes 9437184 | tf_op jit(solution)/shard_map/all_gather | solution.py:392
  14.1 262.2 %all-gather.11.cloned.1.call-start = ((), (), s32[]{:S(2)}) async-start(), calls=%async_computation.10 | async-start | bytes 18874368 | tf_op jit(solution)/shard_map/all_gather | solution.py:392
  183.1 38.7 %all-to-all-start = ((bf16[8,512,256]{1,2,0:T(8,128)(2,1)}), bf16[8,512,256]{1,2,0:T(8,128)(2,1)}, u32[]{:S(2)}, u32[]{:S(2)}) async-start(bf16[8,512,256]{1,2,0:T(8,128)(2,1)} %copy.33), calls=%async_computation | async-start | bytes 4194304 | tf_op jit(solution)/shard_map/all_to_all | solution.py:412
  187.4 181.0 %all-gather.9.cloned.1.call-start = ((), (), s32[]{:S(2)}) async-start(), calls=%async_computation.9 | async-start | bytes 18874368 | tf_op jit(solution)/shard_map/all_gather | solution.py:392
  233.3 356.1 %reduce-scatter.10.cloned.1.call-start = ((), (), s32[]{:S(2)}) async-start(), calls=%async_computation.12 | async-start | bytes 18874368 | tf_op jit(solution)/shard_map/reduce_scatter | solution.py:395
  473.1 287.1 %reduce-scatter.8.cloned.1.call-start = ((), (), s32[]{:S(2)}) async-start(), calls=%async_computation.11 | async-start | bytes 18874368 | tf_op jit(solution)/shard_map/reduce_scatter | solution.py:395
  497.4 92.0 %copy-start.16 = (f32[2048]{0:T(1024)S(1)}, f32[2048]{0:T(1024)}, u32[]{:S(2)}) copy-start(f32[2048]{0:T(1024)} %param.19) | copy-start | bytes 24580
  497.4 92.0 %copy-start.21 = (f32[512]{0:T(512)S(1)}, f32[512]{0:T(512)}, u32[]{:S(2)}) copy-start(f32[512]{0:T(512)} %copy-done.20) | copy-start | bytes 6148
  497.4 96.1 %copy-start.7 = (bf16[512,2048]{1,0:T(8,128)(2,1)S(1)}, bf16[512,2048]{1,0:T(8,128)(2,1)}, u32[]{:S(2)}) copy-start(bf16[512,2048]{1,0:T(8,128)(2,1)} %param.24) | copy-start | bytes 6291460
  497.5 610.2 %reduce-scatter.14.cloned.1.call-start = ((), (), s32[]{:S(2)}) async-start(), calls=%async_computation.14 | async-start | bytes 9437184 | tf_op jit(solution)/shard_map/reduce_scatter | solution.py:395
  620.1 48.7 %all-to-all-start.1 = ((bf16[512,8,256]{2,0,1:T(8,128)(2,1)}), bf16[512,8,256]{2,0,1:T(8,128)(2,1)S(1)}, u32[]{:S(2)}, u32[]{:S(2)}) async-start(bf16[512,8,256]{2,0,1:T(8,128)(2,1)} %bitcast.34), calls=%async_computation.3 | async-start | bytes 4194304 | tf_op jit(solution)/shard_map/all_to_all | solution.py:428
  623.7 589.5 %reduce-scatter.16.cloned.1.call-start = ((), (), s32[]{:S(2)}) async-start(), calls=%async_computation.15 | async-start | bytes 1179648
  782.4 692.7 %reduce-scatter.12.cloned.1.call-start = ((), (), s32[]{:S(2)}) async-start(), calls=%async_computation.13 | async-start | bytes 18874368 | tf_op jit(solution)/shard_map/reduce_scatter | solution.py:395
  825.5 92.2 %collective-permute-start.9 = (bf16[2048,1024]{1,0:T(8,128)(2,1)S(1)}, bf16[2048,1024]{1,0:T(8,128)(2,1)}, u32[]{:S(2)}, u32[]{:S(2)}) collective-permute-start(bf16[2048,1024]{1,0:T(8,128)(2,1)S(1)} %fusion.22), channel_id=1, source_target_pairs={{0,8},{24,16},{1,9},{25,17},{2,10},{26,18},{3,11},{27,19},{4,12},{... | collective-permute-start | bytes 12582920 | tf_op jit(solution)/shard_map/ppermute | solution.py:355
  851.8 155.8 %collective-permute-start.12 = (bf16[2048,1024]{1,0:T(8,128)(2,1)S(1)}, bf16[2048,1024]{1,0:T(8,128)(2,1)}, u32[]{:S(2)}, u32[]{:S(2)}) collective-permute-start(bf16[2048,1024]{1,0:T(8,128)(2,1)S(1)} %fusion.25), channel_id=1, source_target_pairs={{0,8},{24,16},{1,9},{25,17},{2,10},{26,18},{3,11},{27,19},{4,12},{... | collective-permute-start | bytes 12582920 | tf_op jit(solution)/shard_map/ppermute | solution.py:355
  880.7 212.6 %collective-permute-start.15 = (bf16[1024,2048]{1,0:T(8,128)(2,1)S(1)}, bf16[1024,2048]{1,0:T(8,128)(2,1)S(1)}, u32[]{:S(2)}, u32[]{:S(2)}) collective-permute-start(bf16[1024,2048]{1,0:T(8,128)(2,1)S(1)} %convolution_convert_fusion.4), channel_id=1, source_target_pairs={{0,8},{24,16},{1,9},{25,17},{2,10},{26,18},{3,11},{27,19},{4,12},{... | collective-permute-start | bytes 12582920 | tf_op jit(solution)/shard_map/ppermute | solution.py:355
  923.6 176.5 %collective-permute-start.10 = (bf16[2048,1024]{1,0:T(8,128)(2,1)S(1)}, bf16[2048,1024]{1,0:T(8,128)(2,1)}, u32[]{:S(2)}, u32[]{:S(2)}) collective-permute-start(bf16[2048,1024]{1,0:T(8,128)(2,1)S(1)} %add.89), channel_id=1, source_target_pairs={{8,16},{16,8},{9,17},{17,9},{10,18},{18,10},{11,19},{19,11},{12,20... | collective-permute-start | bytes 12582920 | tf_op jit(solution)/shard_map/ppermute | solution.py:355
  1013.9 104.4 %collective-permute-start.13 = (bf16[2048,1024]{1,0:T(8,128)(2,1)}, bf16[2048,1024]{1,0:T(8,128)(2,1)}, u32[]{:S(2)}, u32[]{:S(2)}) collective-permute-start(bf16[2048,1024]{1,0:T(8,128)(2,1)} %add.91), channel_id=1, source_target_pairs={{8,16},{16,8},{9,17},{17,9},{10,18},{18,10},{11,19},{19,11},{12,20... | collective-permute-start | bytes 12582920 | tf_op jit(solution)/shard_map/ppermute | solution.py:355
  1097.4 36.5 %collective-permute-start.16 = (bf16[1024,2048]{1,0:T(8,128)(2,1)}, bf16[1024,2048]{1,0:T(8,128)(2,1)}, u32[]{:S(2)}, u32[]{:S(2)}) collective-permute-start(bf16[1024,2048]{1,0:T(8,128)(2,1)} %add.93), channel_id=1, source_target_pairs={{8,16},{16,8},{9,17},{17,9},{10,18},{18,10},{11,19},{19,11},{12,20... | collective-permute-start | bytes 12582920 | tf_op jit(solution)/shard_map/ppermute | solution.py:355
  1106.3 100.7 %collective-permute-start.11 = (bf16[2048,1024]{1,0:T(8,128)(2,1)}, bf16[2048,1024]{1,0:T(8,128)(2,1)}, u32[]{:S(2)}, u32[]{:S(2)}) collective-permute-start(bf16[2048,1024]{1,0:T(8,128)(2,1)} %add.90), channel_id=1, source_target_pairs={{8,0},{16,24},{9,1},{17,25},{10,2},{18,26},{11,3},{19,27},{12,4},{... | collective-permute-start | bytes 12582920 | tf_op jit(solution)/shard_map/ppermute | solution.py:355
  1111.6 52.5 %collective-permute-start.3 = (bf16[1024,1024]{1,0:T(8,128)(2,1)S(1)}, bf16[1024,1024]{1,0:T(8,128)(2,1)S(1)}, u32[]{:S(2)}, u32[]{:S(2)}) collective-permute-start(bf16[1024,1024]{1,0:T(8,128)(2,1)S(1)} %get-tuple-element.35), channel_id=1, source_target_pairs={{0,8},{24,16},{1,9},{25,17},{2,10},{26,18},{3,11},{27,19},{4,12},{... | collective-permute-start | bytes 6291464 | tf_op jit(solution)/shard_map/ppermute | solution.py:355
  1125.9 166.0 %collective-permute-start.14 = (bf16[2048,1024]{1,0:T(8,128)(2,1)}, bf16[2048,1024]{1,0:T(8,128)(2,1)}, u32[]{:S(2)}, u32[]{:S(2)}) collective-permute-start(bf16[2048,1024]{1,0:T(8,128)(2,1)} %add.92), channel_id=1, source_target_pairs={{8,0},{16,24},{9,1},{17,25},{10,2},{18,26},{11,3},{19,27},{12,4},{... | collective-permute-start | bytes 12582920 | tf_op jit(solution)/shard_map/ppermute | solution.py:355
  1127.2 76.6 %collective-permute-start.6 = (bf16[1024,1024]{1,0:T(8,128)(2,1)S(1)}, bf16[1024,1024]{1,0:T(8,128)(2,1)S(1)}, u32[]{:S(2)}, u32[]{:S(2)}) collective-permute-start(bf16[1024,1024]{1,0:T(8,128)(2,1)S(1)} %get-tuple-element.36), channel_id=1, source_target_pairs={{0,8},{24,16},{1,9},{25,17},{2,10},{26,18},{3,11},{27,19},{4,12},{... | collective-permute-start | bytes 6291464 | tf_op jit(solution)/shard_map/ppermute | solution.py:355
  1141.7 240.0 %collective-permute-start.17 = (bf16[1024,2048]{1,0:T(8,128)(2,1)}, bf16[1024,2048]{1,0:T(8,128)(2,1)}, u32[]{:S(2)}, u32[]{:S(2)}) collective-permute-start(bf16[1024,2048]{1,0:T(8,128)(2,1)} %add.94), channel_id=1, source_target_pairs={{8,0},{16,24},{9,1},{17,25},{10,2},{18,26},{11,3},{19,27},{12,4},{... | collective-permute-start | bytes 12582920 | tf_op jit(solution)/shard_map/ppermute | solution.py:355
  1166.5 55.8 %collective-permute-start.4 = (bf16[1024,1024]{1,0:T(8,128)(2,1)}, bf16[1024,1024]{1,0:T(8,128)(2,1)}, u32[]{:S(2)}, u32[]{:S(2)}) collective-permute-start(bf16[1024,1024]{1,0:T(8,128)(2,1)} %add.85), channel_id=1, source_target_pairs={{8,16},{16,8},{9,17},{17,9},{10,18},{18,10},{11,19},{19,11},{12,20... | collective-permute-start | bytes 6291464 | tf_op jit(solution)/shard_map/ppermute | solution.py:355
  1204.8 93.9 %collective-permute-start.7 = (bf16[1024,1024]{1,0:T(8,128)(2,1)S(1)}, bf16[1024,1024]{1,0:T(8,128)(2,1)}, u32[]{:S(2)}, u32[]{:S(2)}) collective-permute-start(bf16[1024,1024]{1,0:T(8,128)(2,1)S(1)} %add.87), channel_id=1, source_target_pairs={{8,16},{16,8},{9,17},{17,9},{10,18},{18,10},{11,19},{19,11},{12,20... | collective-permute-start | bytes 6291464 | tf_op jit(solution)/shard_map/ppermute | solution.py:355
  1214.2 83.8 %collective-permute-start = (f32[2,256]{1,0:T(2,128)S(1)}, f32[2,256]{1,0:T(2,128)S(1)}, u32[]{:S(2)}, u32[]{:S(2)}) collective-permute-start(f32[2,256]{1,0:T(2,128)S(1)} %copy.38), channel_id=1, source_target_pairs={{0,8},{24,16},{1,9},{25,17},{2,10},{26,18},{3,11},{27,19},{4,12},{... | collective-permute-start | bytes 6152 | tf_op jit(solution)/shard_map/ppermute | solution.py:355
  1225.5 241.6 %collective-permute-start.5 = (bf16[1024,1024]{1,0:T(8,128)(2,1)S(1)}, bf16[1024,1024]{1,0:T(8,128)(2,1)S(1)}, u32[]{:S(2)}, u32[]{:S(2)}) collective-permute-start(bf16[1024,1024]{1,0:T(8,128)(2,1)S(1)} %add.86), channel_id=1, source_target_pairs={{8,0},{16,24},{9,1},{17,25},{10,2},{18,26},{11,3},{19,27},{12,4},{... | collective-permute-start | bytes 6291464 | tf_op jit(solution)/shard_map/ppermute | solution.py:355
  1298.0 89.9 %collective-permute-start.1 = (f32[2,256]{1,0:T(2,128)S(1)}, f32[2,256]{1,0:T(2,128)S(1)}, u32[]{:S(2)}, u32[]{:S(2)}) collective-permute-start(f32[2,256]{1,0:T(2,128)S(1)} %add.83), channel_id=1, source_target_pairs={{8,16},{16,8},{9,17},{17,9},{10,18},{18,10},{11,19},{19,11},{12,20... | collective-permute-start | bytes 6152 | tf_op jit(solution)/shard_map/ppermute | solution.py:355
  1301.2 166.1 %collective-permute-start.8 = (bf16[1024,1024]{1,0:T(8,128)(2,1)S(1)}, bf16[1024,1024]{1,0:T(8,128)(2,1)S(1)}, u32[]{:S(2)}, u32[]{:S(2)}) collective-permute-start(bf16[1024,1024]{1,0:T(8,128)(2,1)S(1)} %add.88), channel_id=1, source_target_pairs={{8,0},{16,24},{9,1},{17,25},{10,2},{18,26},{11,3},{19,27},{12,4},{... | collective-permute-start | bytes 6291464 | tf_op jit(solution)/shard_map/ppermute | solution.py:355
  1387.9 78.6 %collective-permute-start.2 = (f32[2,256]{1,0:T(2,128)S(1)}, f32[2,256]{1,0:T(2,128)S(1)}, u32[]{:S(2)}, u32[]{:S(2)}) collective-permute-start(f32[2,256]{1,0:T(2,128)S(1)} %add.84), channel_id=1, source_target_pairs={{8,0},{16,24},{9,1},{17,25},{10,2},{18,26},{11,3},{19,27},{12,4},{... | collective-permute-start | bytes 6152 | tf_op jit(solution)/shard_map/ppermute | solution.py:355
  (19 other events, 316.9 us)
Sparse Core Ops, SparseCore 0:
  13.5 92.4 all-gather.4
  107.9 54.2 all-gather.6
  164.1 112.1 all-gather.10
  278.6 89.7 all-gather.8
  473.2 116.1 reduce-scatter.9
  592.9 134.2 reduce-scatter.7
  731.2 71.4 reduce-scatter.13
  806.5 35.9 reduce-scatter.15
  846.0 116.1 reduce-scatter.11
where the time goes:
time: 1500 us; the launch traced here: 1490 us
  waiting for transfers between devices  846 us (56%)
  Pallas kernels  226 us (15%)
  matrix products  205 us (14%)
  other arithmetic  108 us (7%)
  starting transfers between devices  60.4 us (4%)
  local copies, waits for them, and re-layouts  29.5 us (2%)
    ppermute x18, waiting for transfers between devices, hop(): return lax.ppermute(piece, 'dp', moves)  469 us
    all_gather x4, waiting for transfers between devices, gather(): return lax.all_gather(value, 'tensor', axis=0, tiled=True)  208 us
    dot_general x10, matrix products, mm(): return lax.dot_general(a, b, dims, preferred_element_type=f32)  205 us
    reduce_scatter x4, waiting for transfers between devices, scatter(): return lax.psum_scatter(value, 'tensor', scatter_dimension=0, tiled=True)  92 us
    pallas_call x2, Pallas kernels, attend_backward(): pl.pallas_call(body, grid_spec=pltpu.PrefetchScalarGridSpec(num_scalar_pr...  90 us
    pallas_call x1, Pallas kernels, mlp_middle(): pl.pallas_call(mlp_kernel, grid=(count // block,), in_specs=[pl.BlockSpec...  62.6 us
    pallas_call x1, Pallas kernels, attend_forward(): pl.pallas_call(functools.partial(forward_kernel, bk), grid_spec=pltpu.Pre...  53 us
    ppermute x18, starting transfers between devices, hop(): return lax.ppermute(piece, 'dp', moves)  51.2 us
  transfers between devices with their start and end apart: 29, of which 14 were waited for; matrix products, arithmetic and copies ran while one was open for 19% of the time, Pallas kernels for 11%

commit v1 on v0

--- a/solution.py
+++ b/solution.py
@@ -30,31 +30,28 @@
 
 
 def turn(values, cosine, sine):
-    width = cosine.shape[-1]
-    parts = []
-    for start in range(0, values.shape[-1], width):
-        piece = values[:, start : start + width]
-        parts.append(piece * cosine + swap_halves(piece) * sine)
-    return parts[0] if len(parts) == 1 else jnp.concatenate(parts, axis=1)
+    return values * cosine + swap_halves(values) * sine
 
 
 def turn_back(values, cosine, sine):
-    width = cosine.shape[-1]
-    parts = []
-    for start in range(0, values.shape[-1], width):
-        piece = values[:, start : start + width]
-        parts.append(piece * cosine + swap_halves(piece * sine))
-    return parts[0] if len(parts) == 1 else jnp.concatenate(parts, axis=1)
+    return values * cosine + swap_halves(values * sine)
+
+
+def group_width(width):
+    return min(2 * HD, width)
 
 
 def qkv_kernel(x_ref, w_ref, cos_ref, sin_ref, q_ref, k_ref, v_ref):
-    width = q_ref.shape[1]
+    size = group_width(q_ref.shape[1])
     projected = jnp.dot(x_ref[...], w_ref[...], preferred_element_type=jnp.float32)
     cosine, sine = cos_ref[...], sin_ref[...]
-    turned = turn(projected[:, :width], cosine, sine).astype(jnp.bfloat16)
-    q_ref[...] = turned * jnp.bfloat16(HD**-0.5)
-    k_ref[...] = turn(projected[:, width : 2 * width], cosine, sine).astype(jnp.bfloat16)
-    v_ref[...] = projected[:, 2 * width :].astype(jnp.bfloat16)
+    for start in range(0, q_ref.shape[1], size):
+        part = lambda n: projected[:, 3 * start + n * size : 3 * start + (n + 1) * size]
+        mine = slice(start, start + size)
+        turned = turn(part(0), cosine, sine).astype(jnp.bfloat16)
+        q_ref[:, mine] = turned * jnp.bfloat16(HD**-0.5)
+        k_ref[:, mine] = turn(part(1), cosine, sine).astype(jnp.bfloat16)
+        v_ref[:, mine] = part(2).astype(jnp.bfloat16)
 
 
 def project(tokens, joined_w, cosine, sine):
@@ -172,7 +169,7 @@
 
 
 def backward_kernel(
-    bk, bq, low_ref, q_ref, k_ref, v_ref, o_ref, do_ref, lse_ref, pos_ref, cos_ref, sin_ref, out_ref,
+    first_head, bk, bq, low_ref, q_ref, k_ref, v_ref, o_ref, do_ref, lse_ref, pos_ref, cos_ref, sin_ref, out_ref,
     kt, dqt, dk, dv,
 ):
     row, i = pl.program_id(0), pl.program_id(1)
@@ -199,7 +196,7 @@
     centre = lax.dot_general(
         pick, products, NT, precision=lax.Precision.HIGHEST, preferred_element_type=jnp.float32
     )
-    level = lse_ref[0, :, here]
+    level = lse_ref[0, first_head : first_head + heads, here]
     q_index = i * bq + lax.broadcasted_iota(jnp.int32, (1, bq), 1)
     first = q_index - pos_ref[0, :, here]
     dqt[...] = jnp.zeros_like(dqt)
@@ -240,35 +237,28 @@
         out_ref[:, 2 * width : 3 * width] = dv[...].astype(jnp.bfloat16)
 
 
-def attend_backward(row, so_far, q, k, v, o, d_o, lse, positions, cosine, sine, bq, bk):
+def attend_backward(group, q, k, v, o, d_o, lse, positions, cosine, sine, bq, bk):
     rows, length = positions.shape
-    width = q.shape[1]
+    width = group_width(q.shape[1])
     per = length // bq
     starts = jnp.arange(0, length, bq, dtype=jnp.int32)
-    low = (starts[None, :] - positions[row : row + 1, ::bq]) // bk
+    low = (starts[None, :] - positions[:, ::bq]) // bk
     pos3 = positions[:, None, :]
-    whole = pl.BlockSpec((length, width), lambda r, i, low: (row, 0))
-    table = pl.BlockSpec((length, cosine.shape[1]), lambda r, i, low: (row, 0))
-    arrays = [low, q, k, v, o, d_o, lse, pos3, cosine, sine]
-    specs = [whole] * 5 + [
-        pl.BlockSpec((1, 8, length), lambda r, i, low: (row, 0, 0)),
-        pl.BlockSpec((1, 1, length), lambda r, i, low: (row, 0, 0)),
-        table,
-        table,
-    ]
-    body, alias = functools.partial(backward_kernel, bk, bq), {}
-    if so_far is not None:
-        arrays.append(so_far)
-        specs.append(pl.BlockSpec(memory_space=pl.ANY))
-        alias = {len(arrays) - 1: 0}
-        body = lambda *refs: backward_kernel(bk, bq, *refs[:10], *refs[11:])
+    whole = pl.BlockSpec((length, width), lambda r, i, low: (r, group))
+    table = pl.BlockSpec((length, width), lambda r, i, low: (r, 0))
     return pl.pallas_call(
-        body,
+        functools.partial(backward_kernel, group * (width // HD), bk, bq),
         grid_spec=pltpu.PrefetchScalarGridSpec(
             num_scalar_prefetch=1,
-            grid=(1, per),
-            in_specs=specs,
-            out_specs=pl.BlockSpec((length, 3 * width), lambda r, i, low: (row, 0)),
+            grid=(rows, per),
+            in_specs=[whole] * 5
+            + [
+                pl.BlockSpec((1, 8, length), lambda r, i, low: (r, 0, 0)),
+                pl.BlockSpec((1, 1, length), lambda r, i, low: (r, 0, 0)),
+                table,
+                table,
+            ],
+            out_specs=pl.BlockSpec((length, 3 * width), lambda r, i, low: (r, 0)),
             scratch_shapes=[
                 pltpu.VMEM((width, length), jnp.bfloat16),
                 pltpu.VMEM((width, bq), jnp.float32),
@@ -277,11 +267,10 @@
             ],
         ),
         out_shape=jax.ShapeDtypeStruct((rows * length, 3 * width), jnp.bfloat16),
-        input_output_aliases=alias,
         compiler_params=pltpu.CompilerParams(vmem_limit_bytes=VMEM_MAX),
-        cost_estimate=cost(28 * length * length * width, 20 * length * width),
+        cost_estimate=cost(28 * rows * length * length * width, 20 * rows * length * width),
         name="attend_back",
-    )(*arrays)
+    )(low, q, k, v, o, d_o, lse, pos3, cosine, sine)
 
 
 def mlp_kernel(n_ref, g_ref, wg_ref, wu_ref, wd_ref, hidden_ref, both_ref):
@@ -398,9 +387,15 @@
         return lax.dot_general(a, b, dims, preferred_element_type=f32)
 
     TN = (((0,), (0,)), ((), ()))
-    joined_w = jnp.concatenate([w_query, w_key, w_value], axis=1)
+    size = group_width(hidden_w)
+    groups = range(hidden_w // size)
+    group_w = [
+        jnp.concatenate([w[:, g * size : (g + 1) * size] for w in (w_query, w_key, w_value)], axis=1)
+        for g in groups
+    ]
+    joined_w = jnp.concatenate(group_w, axis=1)
     both_w = jnp.concatenate([w_gate, w_up], axis=1)
-    cosine, sine = rotary_tables(positions.reshape(-1), min(2 * HD, hidden_w))
+    cosine, sine = rotary_tables(positions.reshape(-1), size)
 
     inputs = layer_input.astype(f32)
     unit_one, inverse_one = normalize(inputs)
@@ -415,10 +410,17 @@
     unit_two, inverse_two = normalize(residual)
     all_two = gather((unit_two * gain_mlp).astype(bf16))
     hidden, d_both = mlp_middle(all_two, all_grad, w_gate, w_up, w_down)
-    grad_down = mm(hidden, all_grad, TN).astype(bf16)
+    half_ff, half = ff_local // 2, width // 2
+    grad_down = [
+        mm(hidden[:, :half_ff], all_grad, TN).astype(bf16),
+        mm(hidden[:, half_ff:], all_grad, TN).astype(bf16),
+    ]
     d_two = scatter(mm(d_both, both_w, NT).astype(bf16)).astype(f32)
     grad_gate = mm(all_two, d_both[:, :ff_local], TN).astype(bf16)
-    grad_up = mm(all_two, d_both[:, ff_local:], TN).astype(bf16)
+    grad_up = [
+        mm(all_two[:, :half], d_both[:, ff_local:], TN).astype(bf16),
+        mm(all_two[:, half:], d_both[:, ff_local:], TN).astype(bf16),
+    ]
     layer_sum = scatter(mm(hidden, w_down).astype(bf16))
 
     gain_two_part = jnp.sum(d_two * unit_two, axis=0)
@@ -426,39 +428,46 @@
     d_attn = d_residual.astype(bf16)
     d_mixed = mm(d_attn, all_w_out, NT).astype(bf16)
     d_attended = lax.all_to_all(d_mixed, "tensor", split_axis=1, concat_axis=0, tiled=True)
-    grad_out = scatter(mm(mixed, d_attn, TN).astype(bf16))
-    d_projected = None
-    for row in range(positions.shape[0]):
-        d_projected = attend_backward(
-            row, d_projected, queries, keys, values, attended, d_attended, level, positions,
-            cosine, sine, block, block,
+    grad_out = mm(mixed, d_attn, TN).astype(bf16)
+    d_attended, grad_out = lax.optimization_barrier((d_attended, grad_out))
+    grad_out = scatter(grad_out)
+    d_projected, grad_joined = [], []
+    for g in groups:
+        part = attend_backward(
+            g, queries, keys, values, attended, d_attended, level, positions, cosine, sine,
+            block, block,
         )
-    layer_sum, d_projected = lax.optimization_barrier((layer_sum, d_projected))
+        d_projected.append(part)
+        grad_joined.append(mm(all_one, part, TN).astype(bf16))
+    layer_sum, last = lax.optimization_barrier((layer_sum, d_projected[-1]))
+    d_projected = jnp.concatenate(d_projected[:-1] + [last], axis=1)
     layer_out = (residual + layer_sum.astype(f32)).astype(bf16)
     d_one = scatter(mm(d_projected, joined_w, NT).astype(bf16)).astype(f32)
-    grad_joined = mm(all_one, d_projected, TN).astype(bf16)
-    plain_joined = lax.optimization_barrier(grad_joined)
-    gain_one_part = jnp.sum(plain_joined.astype(f32) * joined_w.astype(f32), axis=1) / gain_attn
+    gain_one_part = sum(
+        jnp.sum(grad.astype(f32) * w.astype(f32), axis=1)
+        for grad, w in zip(lax.optimization_barrier(grad_joined), group_w)
+    ) / gain_attn
     gains = lax.psum_scatter(
         jnp.stack([gain_one_part, gain_two_part]), "tensor", scatter_dimension=1, tiled=True
     )
     gains = sum_over_dp(gains)
     input_grad = d_residual + norm_back(d_one, gain_attn, unit_one, inverse_one)
 
-    down = sum_over_dp(grad_down)
+    over_dp = lambda pieces: [sum_over_dp(p) for p in pieces]
+    down = jnp.concatenate(over_dp(grad_down), axis=0)
     gate = sum_over_dp(grad_gate)
-    up = sum_over_dp(grad_up)
-    rest = jnp.concatenate([grad_joined, grad_out.reshape(width, hidden_w)], axis=1)
-    middle = width // 2
-    rest = jnp.concatenate([sum_over_dp(rest[:middle]), sum_over_dp(rest[middle:])], axis=0)
+    up = jnp.concatenate(over_dp(grad_up), axis=0)
+    joined = over_dp(grad_joined)
+    out = sum_over_dp(grad_out)
+    pick = lambda n: jnp.concatenate([part[:, n * size : (n + 1) * size] for part in joined], axis=1)
     return (
         layer_out,
         input_grad,
         gains[0],
-        rest[:, :hidden_w],
-        rest[:, hidden_w : 2 * hidden_w],
-        rest[:, 2 * hidden_w : 3 * hidden_w],
-        rest[:, 3 * hidden_w :].reshape(hidden_w, width),
+        pick(0),
+        pick(1),
+        pick(2),
+        out,
         gains[1],
         gate,
         up,

time: 1500 us -> 1500 us (level); the launches traced: 1490 us -> 1470 us
  waiting for transfers between devices: 846 us -> 723 us
  starting transfers between devices: 60.4 us -> 153 us
  matrix products: 205 us -> 226 us
    ppermute x18 -> x27, waiting for transfers between devices: 469 us -> 367 us  [hop(): return lax.ppermute(piece, 'dp', moves)]
    ppermute x18 -> x27, starting transfers between devices: 51.2 us -> 144 us  [hop(): return lax.ppermute(piece, 'dp', moves)]
    all_to_all x1, waiting for transfers between devices: 42.1 us -> 21.1 us  [local(): lax.all_to_all(d_mixed, 'tensor', split_axis=1, concat_axis=0, tiled=True)]
    dot_general x10 -> x13, matrix products: 205 us -> 226 us  [mm(): return lax.dot_general(a, b, dims, preferred_element_type=f32)]
    concatenate x2 -> x6, other arithmetic: 2.73 us -> 17.8 us  [the longest x1 6.1 us: local(): up = jnp.concatenate(over_dp(grad_up), axis=0)]
  transfers between devices with their start and end apart: 29 -> 38, of which waited for: 14 -> 16; matrix products, arithmetic and copies ran while one was open for 19% -> 20% of each run, Pallas kernels for 11% -> 11%
where the time goes in v1:
time: 1500 us; the launch traced here: 1470 us
  waiting for transfers between devices  723 us (48%)
  matrix products  226 us (15%)
  Pallas kernels  225 us (15%)
  starting transfers between devices  153 us (10%)
  other arithmetic  112 us (7%)
  local copies, waits for them, and re-layouts  17.6 us (1%)
    ppermute x27, waiting for transfers between devices, hop(): return lax.ppermute(piece, 'dp', moves)  367 us
    dot_general x13, matrix products, mm(): return lax.dot_general(a, b, dims, preferred_element_type=f32)  226 us
    all_gather x4, waiting for transfers between devices, gather(): return lax.all_gather(value, 'tensor', axis=0, tiled=True)  206 us
    ppermute x27, starting transfers between devices, hop(): return lax.ppermute(piece, 'dp', moves)  144 us
    reduce_scatter x4, waiting for transfers between devices, scatter(): return lax.psum_scatter(value, 'tensor', scatter_dimension=0, tiled=True)  92 us
    pallas_call x2, Pallas kernels, attend_backward(): pl.pallas_call(functools.partial(backward_kernel, group * (width // HD),...  89.4 us
    pallas_call x1, Pallas kernels, mlp_middle(): pl.pallas_call(mlp_kernel, grid=(count // block,), in_specs=[pl.BlockSpec...  62.6 us
    pallas_call x1, Pallas kernels, attend_forward(): pl.pallas_call(functools.partial(forward_kernel, bk), grid_spec=pltpu.Pre...  53 us
  transfers between devices with their start and end apart: 38, of which 16 were waited for; matrix products, arithmetic and copies ran while one was open for 20% of the time, Pallas kernels for 11%

profile of v1, /device:TPU:0, one launch (start us, length us, event | category | flops | bytes accessed | tf_op | source)
XLA Modules:
  0.0 1471.6 jit_solution(8207764103557149031)
XLA Ops:
  33.3 71.9 %all-gather.5.cloned.1.call-done.x_ref = bf16[4096,2048]{1,0:T(8,128)(2,1)} async-done(((bf16[512,2048]{1,0:T(8,128)(2,1)}), bf16[4096,2048]{1,0:T(8,128)(2,1)}) %all-gather.5.cloned.1.call-update) | async-done | bytes 16777232 | tf_op jit(solution)/shard_map/all_gather | solution.py:381
  105.2 20.0 %qkv.1 = (bf16[4096,256]{1,0:T(8,128)(2,1)}, bf16[4096,256]{1,0:T(8,128)(2,1)}, bf16[4096,256]{1,0:T(8,128)(2,1)}) custom-call(bf16[4096,2048]{1,0:T(8,128)(2,1)} %all-gather.5.cloned.1.call-done.x_ref, bf16[2048,768]{1,0:T(8,128)(2,1)} %copy-done.26, f32[4096,128]{1,0:T(8,128)} %pad_maximum_fusion.cos_ref, f32[4096,128]{1,0:T(8,128)} %pad_maximum_fusion.1.sin_ref), custom_call_target="tpu_custom_call" | custom-call | flops 12884901888 | bytes 16777216 | tf_op jit(solution)/shard_map/qkv/pallas_call | solution.py:63
  125.2 53.0 %attend.1 = (bf16[4096,256]{1,0:T(8,128)(2,1)}, f32[2,8,2048]{2,1,0:T(8,128)}) custom-call(s32[2,4]{1,0:T(2,128)} %and_select_fusion.low_ref, bf16[4096,256]{1,0:T(8,128)(2,1)} %get-tuple-element.24.q_ref, bf16[4096,256]{1,0:T(8,128)(2,1)} %get-tuple-element.25.k_ref, bf16[4096,256]{1,0:T(8,128)(2,1)} %get-tuple-element.26.v_ref, ...), custom_call_target="tpu_custom_call" | custom-call | flops 34359738368 | bytes 10485760 | tf_op jit(solution)/shard_map/attend/pallas_call | solution.py:139
  186.6 34.3 %all-to-all-done = bf16[8,512,256]{1,2,0:T(8,128)(2,1)} async-done(((bf16[8,512,256]{1,2,0:T(8,128)(2,1)}), bf16[8,512,256]{1,2,0:T(8,128)(2,1)}, u32[]{:S(2)}, u32[]{:S(2)}) %all-to-all-start) | async-done | bytes 2097184 | tf_op jit(solution)/shard_map/all_to_all | solution.py:407
  233.1 42.4 %all-gather.11.cloned.1.call-done.g_ref = bf16[4096,2048]{1,0:T(8,128)(2,1)} async-done(((bf16[512,2048]{1,0:T(8,128)(2,1)}), bf16[4096,2048]{1,0:T(8,128)(2,1)}) %all-gather.11.cloned.1.call-update) | async-done | bytes 16777232 | tf_op jit(solution)/shard_map/all_gather | solution.py:381
  275.5 92.1 %all-gather.9.cloned.1.call-done.n_ref = bf16[4096,2048]{1,0:T(8,128)(2,1)} async-done(((bf16[512,2048]{1,0:T(8,128)(2,1)}), bf16[4096,2048]{1,0:T(8,128)(2,1)}) %all-gather.9.cloned.1.call-update) | async-done | bytes 16777232 | tf_op jit(solution)/shard_map/all_gather | solution.py:381
  367.6 62.6 %mlp_middle.1 = (bf16[4096,1024]{1,0:T(8,128)(2,1)}, bf16[4096,2048]{1,0:T(8,128)(2,1)}) custom-call(bf16[4096,2048]{1,0:T(8,128)(2,1)} %all-gather.9.cloned.1.call-done.n_ref, bf16[4096,2048]{1,0:T(8,128)(2,1)} %all-gather.11.cloned.1.call-done.g_ref, bf16[2048,1024]{1,0:T(8,128)(2,1)} %wg_ref.1, bf16[2048,1024]{1,0:T(8,128)(2,1)} %wu_ref.1, ...), custom_call_target="tpu_custom_call" | custom-call | flops 51539607552 | bytes 33554432 | tf_op jit(solution)/shard_map/mlp_middle/pallas_call | solution.py:296
  430.2 42.0 %convolution_convert_fusion.2 = bf16[4096,2048]{1,0:T(8,128)(2,1)} fusion(bf16[4096,2048]{1,0:T(8,128)(2,1)} %get-tuple-element.29, bf16[2048,1024]{1,0:T(8,128)(2,1)} %wu_ref.1, bf16[2048,1024]{1,0:T(8,128)(2,1)} %wg_ref.1), kind=kOutput, calls=%fused_computation.2 | convolution fusion | flops 34384904192 | bytes 41943040 | tf_op jit(solution)/shard_map/dot_general | solution.py:387
  472.3 24.3 %convolution_convert_fusion.1 = bf16[4096,2048]{1,0:T(8,128)(2,1)} fusion(bf16[4096,1024]{1,0:T(8,128)(2,1)} %get-tuple-element.28, bf16[1024,2048]{1,0:T(8,128)(2,1)} %wd_ref.1), kind=kOutput, calls=%fused_computation.1 | convolution fusion | flops 17188257792 | bytes 29360128 | tf_op jit(solution)/shard_map/dot_general | solution.py:387
  496.6 92.0 %reduce-scatter.10.cloned.1.call-done = bf16[512,2048]{1,0:T(8,128)(2,1)} async-done(((bf16[4096,2048]{1,0:T(8,128)(2,1)}), bf16[512,2048]{1,0:T(8,128)(2,1)}) %reduce-scatter.10.cloned.1.call-update) | async-done | bytes 2097168 | tf_op jit(solution)/shard_map/reduce_scatter | solution.py:384
  623.3 21.1 %all-to-all-done.1 = bf16[512,8,256]{2,0,1:T(8,128)(2,1)S(1)} async-done(((bf16[512,8,256]{2,0,1:T(8,128)(2,1)}), bf16[512,8,256]{2,0,1:T(8,128)(2,1)S(1)}, u32[]{:S(2)}, u32[]{:S(2)}) %all-to-all-start.1) | async-done | bytes 2097184 | tf_op jit(solution)/shard_map/all_to_all | solution.py:430
  645.7 44.7 %attend_back.2 = bf16[4096,384]{1,0:T(8,128)(2,1)} custom-call(s32[2,4]{1,0:T(2,128)} %and_select_fusion.low_ref, bf16[4096,256]{1,0:T(8,128)(2,1)} %get-tuple-element.24.q_ref, bf16[4096,256]{1,0:T(8,128)(2,1)} %get-tuple-element.25.k_ref, bf16[4096,256]{1,0:T(8,128)(2,1)} %get-tuple-element.26.v_ref, bf16[4096,256]{1,0:T(8,128)(2,1)} %get-tuple-element.27.o_ref, ...), custom_call_target="tpu_custom_call" | custom-call | flops 30064771072 | bytes 10485760 | tf_op jit(solution)/shard_map/attend_back/pallas_call | solution.py:249
  690.4 14.2 convolution_convert_fusion.5
  704.6 44.7 %attend_back.3 = bf16[4096,384]{1,0:T(8,128)(2,1)} custom-call(s32[2,4]{1,0:T(2,128)} %and_select_fusion.low_ref, bf16[4096,256]{1,0:T(8,128)(2,1)} %get-tuple-element.24.q_ref, bf16[4096,256]{1,0:T(8,128)(2,1)} %get-tuple-element.25.k_ref, bf16[4096,256]{1,0:T(8,128)(2,1)} %get-tuple-element.26.v_ref, bf16[4096,256]{1,0:T(8,128)(2,1)} %get-tuple-element.27.o_ref, ...), custom_call_target="tpu_custom_call" | custom-call | flops 30064771072 | bytes 10485760 | tf_op jit(solution)/shard_map/attend_back/pallas_call | solution.py:249
  749.4 14.6 convolution_convert_fusion.6
  768.7 20.3 %convolution_convert_fusion = bf16[4096,2048]{1,0:T(8,128)(2,1)} fusion(bf16[2048,768]{1,0:T(8,128)(2,1)} %copy-done.26, bf16[4096,384]{1,0:T(8,128)(2,1)} %attend_back.2, bf16[4096,384]{1,0:T(8,128)(2,1)} %attend_back.3), kind=kOutput, calls=%fused_computation | convolution fusion | flops 12905873408 | bytes 26214400 | tf_op jit(solution)/shard_map/dot_general | solution.py:387
  789.1 13.8 fusion.42
  805.5 23.8 %fusion.33 = bf16[2048,1024]{1,0:T(8,128)(2,1)S(1)} fusion(bf16[4096,2048]{1,0:T(8,128)(2,1)} %all-gather.9.cloned.1.call-done.n_ref, bf16[4096,2048]{1,0:T(8,128)(2,1)} %get-tuple-element.29), kind=kOutput, calls=%fused_computation.49 | convolution fusion | flops 17181966336 | bytes 29360128 | tf_op jit(solution)/shard_map/dot_general | solution.py:387
  830.9 13.8 fusion.47
  846.1 14.7 %fusion.36 = bf16[512,2048]{1,0:T(8,128)(2,1)} fusion(bf16[4096,2048]{1,0:T(8,128)(2,1)} %all-gather.11.cloned.1.call-done.g_ref, bf16[4096,1024]{1,0:T(8,128)(2,1)} %get-tuple-element.28), kind=kOutput, calls=%fused_computation.54 | convolution fusion | flops 8590983168 | bytes 23068672 | tf_op jit(solution)/shard_map/dot_general | solution.py:387
  863.6 76.5 %collective-permute-done.12 = bf16[2048,1024]{1,0:T(8,128)(2,1)S(1)} collective-permute-done((bf16[2048,1024]{1,0:T(8,128)(2,1)S(1)}, bf16[2048,1024]{1,0:T(8,128)(2,1)S(1)}, u32[]{:S(2)}, u32[]{:S(2)}) %collective-permute-start.12) | collective-permute-done | bytes 4194336 | tf_op jit(solution)/shard_map/ppermute | solution.py:344
  943.3 14.1 fusion.39
  966.1 64.0 %collective-permute-done.21 = bf16[512,2048]{1,0:T(8,128)(2,1)} collective-permute-done((bf16[512,2048]{1,0:T(8,128)(2,1)}, bf16[512,2048]{1,0:T(8,128)(2,1)}, u32[]{:S(2)}, u32[]{:S(2)}) %collective-permute-start.21) | collective-permute-done | bytes 2097184 | tf_op jit(solution)/shard_map/ppermute | solution.py:344
  1036.9 34.3 %collective-permute-done.24 = bf16[512,2048]{1,0:T(8,128)(2,1)S(1)} collective-permute-done((bf16[512,2048]{1,0:T(8,128)(2,1)S(1)}, bf16[512,2048]{1,0:T(8,128)(2,1)S(1)}, u32[]{:S(2)}, u32[]{:S(2)}) %collective-permute-start.24) | collective-permute-done | bytes 2097184 | tf_op jit(solution)/shard_map/ppermute | solution.py:344
  1094.4 30.7 %collective-permute-done.17 = bf16[1024,1024]{1,0:T(8,128)(2,1)S(1)} collective-permute-done((bf16[1024,1024]{1,0:T(8,128)(2,1)S(1)}, bf16[1024,1024]{1,0:T(8,128)(2,1)S(1)}, u32[]{:S(2)}, u32[]{:S(2)}) %collective-permute-start.17) | collective-permute-done | bytes 2097184 | tf_op jit(solution)/shard_map/ppermute | solution.py:344
  1125.1 96.2 %collective-permute-start.3 = (bf16[2048,384]{1,0:T(8,128)(2,1)}, bf16[2048,384]{1,0:T(8,128)(2,1)}, u32[]{:S(2)}, u32[]{:S(2)}) collective-permute-start(bf16[2048,384]{1,0:T(8,128)(2,1)} %convolution_convert_fusion.6), channel_id=1, source_target_pairs={{0,8},{24,16},{1,9},{25,17},{2,10},{26,18},{3,11},{27,19},{4,12},{... | collective-permute-start | bytes 4718600 | tf_op jit(solution)/shard_map/ppermute | solution.py:344
  1227.2 28.0 %collective-permute-done.3 = bf16[2048,384]{1,0:T(8,128)(2,1)} collective-permute-done((bf16[2048,384]{1,0:T(8,128)(2,1)}, bf16[2048,384]{1,0:T(8,128)(2,1)}, u32[]{:S(2)}, u32[]{:S(2)}) %collective-permute-start.3) | collective-permute-done | bytes 1572896 | tf_op jit(solution)/shard_map/ppermute | solution.py:344
  1260.4 19.4 %collective-permute-done.6 = bf16[2048,384]{1,0:T(8,128)(2,1)} collective-permute-done((bf16[2048,384]{1,0:T(8,128)(2,1)}, bf16[2048,384]{1,0:T(8,128)(2,1)}, u32[]{:S(2)}, u32[]{:S(2)}) %collective-permute-start.6) | collective-permute-done | bytes 1572896 | tf_op jit(solution)/shard_map/ppermute | solution.py:344
  1285.0 28.5 %collective-permute-done.20 = bf16[1024,1024]{1,0:T(8,128)(2,1)} collective-permute-done((bf16[1024,1024]{1,0:T(8,128)(2,1)}, bf16[1024,1024]{1,0:T(8,128)(2,1)}, u32[]{:S(2)}, u32[]{:S(2)}) %collective-permute-start.20) | collective-permute-done | bytes 2097184 | tf_op jit(solution)/shard_map/ppermute | solution.py:344
  1316.6 29.0 %collective-permute-done.26 = bf16[512,2048]{1,0:T(8,128)(2,1)} collective-permute-done((bf16[512,2048]{1,0:T(8,128)(2,1)}, bf16[512,2048]{1,0:T(8,128)(2,1)}, u32[]{:S(2)}, u32[]{:S(2)}) %collective-permute-start.26) | collective-permute-done | bytes 2097184 | tf_op jit(solution)/shard_map/ppermute | solution.py:344
  1389.0 35.0 %collective-permute-done.2 = f32[2,256]{1,0:T(2,128)S(1)} collective-permute-done((f32[2,256]{1,0:T(2,128)S(1)}, f32[2,256]{1,0:T(2,128)S(1)}, u32[]{:S(2)}, u32[]{:S(2)}) %collective-permute-start.2) | collective-permute-done | bytes 2080 | tf_op jit(solution)/shard_map/ppermute | solution.py:344
  1434.5 21.1 %collective-permute-done.11 = bf16[256,2048]{1,0:T(8,128)(2,1)S(1)} collective-permute-done((bf16[256,2048]{1,0:T(8,128)(2,1)S(1)}, bf16[256,2048]{1,0:T(8,128)(2,1)S(1)}, u32[]{:S(2)}, u32[]{:S(2)}) %collective-permute-start.11) | collective-permute-done | bytes 1048608 | tf_op jit(solution)/shard_map/ppermute | solution.py:344
  (208 shorter events, 219.4 us)
Async XLA Ops:
  7.2 98.0 %all-gather.5.cloned.1.call-start = ((), (), s32[]{:S(2)}) async-start(), calls=%async_computation.7 | async-start | bytes 18874368 | tf_op jit(solution)/shard_map/all_gather | solution.py:381
  12.6 174.0 %all-gather.7.cloned.1.call-start = ((), (), s32[]{:S(2)}) async-start(), calls=%async_computation.8 | async-start | bytes 9437184 | tf_op jit(solution)/shard_map/all_gather | solution.py:381
  13.3 262.2 %all-gather.11.cloned.1.call-start = ((), (), s32[]{:S(2)}) async-start(), calls=%async_computation.10 | async-start | bytes 18874368 | tf_op jit(solution)/shard_map/all_gather | solution.py:381
  182.2 38.8 %all-to-all-start = ((bf16[8,512,256]{1,2,0:T(8,128)(2,1)}), bf16[8,512,256]{1,2,0:T(8,128)(2,1)}, u32[]{:S(2)}, u32[]{:S(2)}) async-start(bf16[8,512,256]{1,2,0:T(8,128)(2,1)} %copy.35), calls=%async_computation | async-start | bytes 4194304 | tf_op jit(solution)/shard_map/all_to_all | solution.py:407
  186.6 181.0 %all-gather.9.cloned.1.call-start = ((), (), s32[]{:S(2)}) async-start(), calls=%async_computation.9 | async-start | bytes 18874368 | tf_op jit(solution)/shard_map/all_gather | solution.py:381
  233.0 355.6 %reduce-scatter.10.cloned.1.call-start = ((), (), s32[]{:S(2)}) async-start(), calls=%async_computation.12 | async-start | bytes 18874368 | tf_op jit(solution)/shard_map/reduce_scatter | solution.py:384
  472.3 296.5 %reduce-scatter.8.cloned.1.call-start = ((), (), s32[]{:S(2)}) async-start(), calls=%async_computation.11 | async-start | bytes 18874368 | tf_op jit(solution)/shard_map/reduce_scatter | solution.py:384
  611.1 740.7 %reduce-scatter.16.cloned.1.call-start = ((), (), s32[]{:S(2)}) async-start(), calls=%async_computation.15 | async-start | bytes 1179648
  767.9 608.9 %reduce-scatter.14.cloned.1.call-start = ((), (), s32[]{:S(2)}) async-start(), calls=%async_computation.14 | async-start | bytes 9437184 | tf_op jit(solution)/shard_map/reduce_scatter | solution.py:384
  768.7 688.4 %reduce-scatter.12.cloned.1.call-start = ((), (), s32[]{:S(2)}) async-start(), calls=%async_computation.13 | async-start | bytes 18874368 | tf_op jit(solution)/shard_map/reduce_scatter | solution.py:384
  802.9 159.8 %collective-permute-start.15 = (bf16[1024,1024]{1,0:T(8,128)(2,1)S(1)}, bf16[1024,1024]{1,0:T(8,128)(2,1)}, u32[]{:S(2)}, u32[]{:S(2)}) collective-permute-start(bf16[1024,1024]{1,0:T(8,128)(2,1)S(1)} %fusion.42), channel_id=1, source_target_pairs={{0,8},{24,16},{1,9},{25,17},{2,10},{26,18},{3,11},{27,19},{4,12},{... | collective-permute-start | bytes 6291464 | tf_op jit(solution)/shard_map/ppermute | solution.py:344
  829.3 110.8 %collective-permute-start.12 = (bf16[2048,1024]{1,0:T(8,128)(2,1)S(1)}, bf16[2048,1024]{1,0:T(8,128)(2,1)S(1)}, u32[]{:S(2)}, u32[]{:S(2)}) collective-permute-start(bf16[2048,1024]{1,0:T(8,128)(2,1)S(1)} %fusion.33), channel_id=1, source_target_pairs={{0,8},{24,16},{1,9},{25,17},{2,10},{26,18},{3,11},{27,19},{4,12},{... | collective-permute-start | bytes 12582920 | tf_op jit(solution)/shard_map/ppermute | solution.py:344
  844.7 189.2 %collective-permute-start.18 = (bf16[1024,1024]{1,0:T(8,128)(2,1)S(1)}, bf16[1024,1024]{1,0:T(8,128)(2,1)S(1)}, u32[]{:S(2)}, u32[]{:S(2)}) collective-permute-start(bf16[1024,1024]{1,0:T(8,128)(2,1)S(1)} %fusion.47), channel_id=1, source_target_pairs={{0,8},{24,16},{1,9},{25,17},{2,10},{26,18},{3,11},{27,19},{4,12},{... | collective-permute-start | bytes 6291464 | tf_op jit(solution)/shard_map/ppermute | solution.py:344
  860.9 169.2 %collective-permute-start.21 = (bf16[512,2048]{1,0:T(8,128)(2,1)}, bf16[512,2048]{1,0:T(8,128)(2,1)}, u32[]{:S(2)}, u32[]{:S(2)}) collective-permute-start(bf16[512,2048]{1,0:T(8,128)(2,1)} %fusion.36), channel_id=1, source_target_pairs={{0,8},{24,16},{1,9},{25,17},{2,10},{26,18},{3,11},{27,19},{4,12},{... | collective-permute-start | bytes 6291464 | tf_op jit(solution)/shard_map/ppermute | solution.py:344
  942.3 136.4 %collective-permute-start.13 = (bf16[2048,1024]{1,0:T(8,128)(2,1)S(1)}, bf16[2048,1024]{1,0:T(8,128)(2,1)S(1)}, u32[]{:S(2)}, u32[]{:S(2)}) collective-permute-start(bf16[2048,1024]{1,0:T(8,128)(2,1)S(1)} %add.111), channel_id=1, source_target_pairs={{8,16},{16,8},{9,17},{17,9},{10,18},{18,10},{11,19},{19,11},{12,20... | collective-permute-start | bytes 12582920 | tf_op jit(solution)/shard_map/ppermute | solution.py:344
  957.3 113.8 %collective-permute-start.24 = (bf16[512,2048]{1,0:T(8,128)(2,1)S(1)}, bf16[512,2048]{1,0:T(8,128)(2,1)S(1)}, u32[]{:S(2)}, u32[]{:S(2)}) collective-permute-start(bf16[512,2048]{1,0:T(8,128)(2,1)S(1)} %fusion.39), channel_id=1, source_target_pairs={{0,8},{24,16},{1,9},{25,17},{2,10},{26,18},{3,11},{27,19},{4,12},{... | collective-permute-start | bytes 6291464 | tf_op jit(solution)/shard_map/ppermute | solution.py:344
  965.3 108.8 %collective-permute-start.16 = (bf16[1024,1024]{1,0:T(8,128)(2,1)S(1)}, bf16[1024,1024]{1,0:T(8,128)(2,1)S(1)}, u32[]{:S(2)}, u32[]{:S(2)}) collective-permute-start(bf16[1024,1024]{1,0:T(8,128)(2,1)S(1)} %add.113), channel_id=1, source_target_pairs={{8,16},{16,8},{9,17},{17,9},{10,18},{18,10},{11,19},{19,11},{12,20... | collective-permute-start | bytes 6291464 | tf_op jit(solution)/shard_map/ppermute | solution.py:344
  1033.1 43.5 %collective-permute-start.22 = (bf16[512,2048]{1,0:T(8,128)(2,1)S(1)}, bf16[512,2048]{1,0:T(8,128)(2,1)S(1)}, u32[]{:S(2)}, u32[]{:S(2)}) collective-permute-start(bf16[512,2048]{1,0:T(8,128)(2,1)S(1)} %add.117), channel_id=1, source_target_pairs={{8,16},{16,8},{9,17},{17,9},{10,18},{18,10},{11,19},{19,11},{12,20... | collective-permute-start | bytes 6291464 | tf_op jit(solution)/shard_map/ppermute | solution.py:344
  1034.9 49.3 %collective-permute-start.19 = (bf16[1024,1024]{1,0:T(8,128)(2,1)S(1)}, bf16[1024,1024]{1,0:T(8,128)(2,1)}, u32[]{:S(2)}, u32[]{:S(2)}) collective-permute-start(bf16[1024,1024]{1,0:T(8,128)(2,1)S(1)} %add.115), channel_id=1, source_target_pairs={{8,16},{16,8},{9,17},{17,9},{10,18},{18,10},{11,19},{19,11},{12,20... | collective-permute-start | bytes 6291464 | tf_op jit(solution)/shard_map/ppermute | solution.py:344
  1075.0 50.0 %collective-permute-start.17 = (bf16[1024,1024]{1,0:T(8,128)(2,1)S(1)}, bf16[1024,1024]{1,0:T(8,128)(2,1)S(1)}, u32[]{:S(2)}, u32[]{:S(2)}) collective-permute-start(bf16[1024,1024]{1,0:T(8,128)(2,1)S(1)} %add.114), channel_id=1, source_target_pairs={{8,0},{16,24},{9,1},{17,25},{10,2},{18,26},{11,3},{19,27},{12,4},{... | collective-permute-start | bytes 6291464 | tf_op jit(solution)/shard_map/ppermute | solution.py:344
  1077.4 143.9 %collective-permute-start.23 = (bf16[512,2048]{1,0:T(8,128)(2,1)S(1)}, bf16[512,2048]{1,0:T(8,128)(2,1)S(1)}, u32[]{:S(2)}, u32[]{:S(2)}) collective-permute-start(bf16[512,2048]{1,0:T(8,128)(2,1)S(1)} %add.118), channel_id=1, source_target_pairs={{8,0},{16,24},{9,1},{17,25},{10,2},{18,26},{11,3},{19,27},{12,4},{... | collective-permute-start | bytes 6291464 | tf_op jit(solution)/shard_map/ppermute | solution.py:344
  1082.9 286.4 %collective-permute-start.14 = (bf16[2048,1024]{1,0:T(8,128)(2,1)}, bf16[2048,1024]{1,0:T(8,128)(2,1)}, u32[]{:S(2)}, u32[]{:S(2)}) collective-permute-start(bf16[2048,1024]{1,0:T(8,128)(2,1)} %add.112), channel_id=1, source_target_pairs={{8,0},{16,24},{9,1},{17,25},{10,2},{18,26},{11,3},{19,27},{12,4},{... | collective-permute-start | bytes 12582920 | tf_op jit(solution)/shard_map/ppermute | solution.py:344
  1088.1 225.4 %collective-permute-start.20 = (bf16[1024,1024]{1,0:T(8,128)(2,1)}, bf16[1024,1024]{1,0:T(8,128)(2,1)}, u32[]{:S(2)}, u32[]{:S(2)}) collective-permute-start(bf16[1024,1024]{1,0:T(8,128)(2,1)} %add.116), channel_id=1, source_target_pairs={{8,0},{16,24},{9,1},{17,25},{10,2},{18,26},{11,3},{19,27},{12,4},{... | collective-permute-start | bytes 6291464 | tf_op jit(solution)/shard_map/ppermute | solution.py:344
  1093.1 252.6 %collective-permute-start.26 = (bf16[512,2048]{1,0:T(8,128)(2,1)}, bf16[512,2048]{1,0:T(8,128)(2,1)}, u32[]{:S(2)}, u32[]{:S(2)}) collective-permute-start(bf16[512,2048]{1,0:T(8,128)(2,1)} %add.120), channel_id=1, source_target_pairs={{8,0},{16,24},{9,1},{17,25},{10,2},{18,26},{11,3},{19,27},{12,4},{... | collective-permute-start | bytes 6291464 | tf_op jit(solution)/shard_map/ppermute | solution.py:344
  1125.1 130.1 %collective-permute-start.3 = (bf16[2048,384]{1,0:T(8,128)(2,1)}, bf16[2048,384]{1,0:T(8,128)(2,1)}, u32[]{:S(2)}, u32[]{:S(2)}) collective-permute-start(bf16[2048,384]{1,0:T(8,128)(2,1)} %convolution_convert_fusion.6), channel_id=1, source_target_pairs={{0,8},{24,16},{1,9},{25,17},{2,10},{26,18},{3,11},{27,19},{4,12},{... | collective-permute-start | bytes 4718600 | tf_op jit(solution)/shard_map/ppermute | solution.py:344
  1221.3 58.5 %collective-permute-start.6 = (bf16[2048,384]{1,0:T(8,128)(2,1)}, bf16[2048,384]{1,0:T(8,128)(2,1)}, u32[]{:S(2)}, u32[]{:S(2)}) collective-permute-start(bf16[2048,384]{1,0:T(8,128)(2,1)} %convolution_convert_fusion.5), channel_id=1, source_target_pairs={{0,8},{24,16},{1,9},{25,17},{2,10},{26,18},{3,11},{27,19},{4,12},{... | collective-permute-start | bytes 4718600 | tf_op jit(solution)/shard_map/ppermute | solution.py:344
  1258.6 102.4 %collective-permute-start.4 = (bf16[2048,384]{1,0:T(8,128)(2,1)}, bf16[2048,384]{1,0:T(8,128)(2,1)}, u32[]{:S(2)}, u32[]{:S(2)}) collective-permute-start(bf16[2048,384]{1,0:T(8,128)(2,1)} %add.105), channel_id=1, source_target_pairs={{8,16},{16,8},{9,17},{17,9},{10,18},{18,10},{11,19},{19,11},{12,20... | collective-permute-start | bytes 4718600 | tf_op jit(solution)/shard_map/ppermute | solution.py:344
  1283.2 81.4 %collective-permute-start.7 = (bf16[2048,384]{1,0:T(8,128)(2,1)}, bf16[2048,384]{1,0:T(8,128)(2,1)}, u32[]{:S(2)}, u32[]{:S(2)}) collective-permute-start(bf16[2048,384]{1,0:T(8,128)(2,1)} %add.107), channel_id=1, source_target_pairs={{8,16},{16,8},{9,17},{17,9},{10,18},{18,10},{11,19},{19,11},{12,20... | collective-permute-start | bytes 4718600 | tf_op jit(solution)/shard_map/ppermute | solution.py:344
  1363.3 62.4 %collective-permute-start.5 = (bf16[2048,384]{1,0:T(8,128)(2,1)S(1)}, bf16[2048,384]{1,0:T(8,128)(2,1)}, u32[]{:S(2)}, u32[]{:S(2)}) collective-permute-start(bf16[2048,384]{1,0:T(8,128)(2,1)S(1)} %add.106), channel_id=1, source_target_pairs={{8,0},{16,24},{9,1},{17,25},{10,2},{18,26},{11,3},{19,27},{12,4},{... | collective-permute-start | bytes 4718600 | tf_op jit(solution)/shard_map/ppermute | solution.py:344
  1368.0 57.7 %collective-permute-start.8 = (bf16[2048,384]{1,0:T(8,128)(2,1)}, bf16[2048,384]{1,0:T(8,128)(2,1)}, u32[]{:S(2)}, u32[]{:S(2)}) collective-permute-start(bf16[2048,384]{1,0:T(8,128)(2,1)} %add.108), channel_id=1, source_target_pairs={{8,0},{16,24},{9,1},{17,25},{10,2},{18,26},{11,3},{19,27},{12,4},{... | collective-permute-start | bytes 4718600 | tf_op jit(solution)/shard_map/ppermute | solution.py:344
  1375.5 48.5 %collective-permute-start.2 = (f32[2,256]{1,0:T(2,128)S(1)}, f32[2,256]{1,0:T(2,128)S(1)}, u32[]{:S(2)}, u32[]{:S(2)}) collective-permute-start(f32[2,256]{1,0:T(2,128)S(1)} %add.104), channel_id=1, source_target_pairs={{8,0},{16,24},{9,1},{17,25},{10,2},{18,26},{11,3},{19,27},{12,4},{... | collective-permute-start | bytes 6152 | tf_op jit(solution)/shard_map/ppermute | solution.py:344
  1376.8 47.8 %collective-permute-start.9 = (bf16[256,2048]{1,0:T(8,128)(2,1)}, bf16[256,2048]{1,0:T(8,128)(2,1)S(1)}, u32[]{:S(2)}, u32[]{:S(2)}) collective-permute-start(bf16[256,2048]{1,0:T(8,128)(2,1)} %reduce-scatter.14.cloned.1.call-done), channel_id=1, source_target_pairs={{0,8},{24,16},{1,9},{25,17},{2,10},{26,18},{3,11},{27,19},{4,12},{... | collective-permute-start | bytes 3145736 | tf_op jit(solution)/shard_map/ppermute | solution.py:344
  (40 other events, 766.9 us)
Sparse Core Ops, SparseCore 0:
  12.7 92.4 all-gather.4
  107.1 54.2 all-gather.6
  163.3 112.1 all-gather.10
  277.8 89.7 all-gather.8
  472.4 116.1 reduce-scatter.9
  592.0 122.4 reduce-scatter.7
  768.0 32.6 reduce-scatter.15
  804.2 71.4 reduce-scatter.13
  879.3 116.1 reduce-scatter.11
